TPU v7x, 128 devices: a whole 4x4x4 slice. The times are simulated.
128 devices in a mesh: shard: 32 (over x, z, core), task: 4 (over y).
Axes of the slice: x: 4, y: 4, z: 4, core: 2. Of those that a mesh axis runs over, the one named last changes fastest.
Arguments:
- task_deltas: bfloat16 [4, 4, 512, 16384], P('task', None, 'shard')
- rank_scores: int32 [4, 4, 512, 16384], P('task', None, 'shard'), may hold values from 0 to 1073741823
- keep_limits: int32 [4, 4, 8], P('task'), may hold values from 268435456 to 805306367
Outputs:
- merged: bfloat16 [4, 512, 16384], P(None, 'shard', 'task')
All inputs are finite; a program needn't handle non-finite values.
Results may differ from a plain program's by a relative error of at most 0.0051.
Values may be sent and summed in bfloat16 or wider, within the bound.
A program may use at most 64 MiB of HBM per device.

v0:
```python
import jax
import jax.numpy as jnp
from jax import lax
from jax.sharding import Mesh
from jax.sharding import PartitionSpec as P

EXPERTS = 8
FF = 16384
SHARD = ("shard_0", "shard_1", "shard_2")


def swapped(value, axis, stride):
    mask = 2**stride
    pairs = [(source, source ^ mask) for source in range(lax.axis_size(axis))]
    return lax.ppermute(value, axis, pairs)


def one_axis_at_a_time(value, axes):
    for axis in axes:
        value = lax.psum(value, axis)
    return value


def split_up(value, dim, size):
    before, after = (value.shape[:dim], value.shape[dim + 1 :])
    return jnp.moveaxis(value.reshape(*before, size, -1, *after), dim, 0)


def summed_on_arrival(value, axis, dim):
    tiles = split_up(value, dim, lax.axis_size(axis))
    arrived = lax.all_to_all(tiles, axis, split_axis=0, concat_axis=0, tiled=True)
    return arrived.sum(axis=0)


def keep_probability(column_sums, grand_sum, row_total):
    column_mean = column_sums / row_total
    grand_mean = grand_sum / (EXPERTS * row_total * FF)
    return (0.2 + 0.7 * column_mean / (column_mean + grand_mean)).astype(jnp.bfloat16)


def on_device(task_deltas, rank_scores, keep_limits):
    groups = lax.axis_size(SHARD) // EXPERTS
    expert = lax.axis_index(SHARD) // groups
    row_count = task_deltas.shape[2]
    rows_whole = row_count * groups
    selector = jnp.arange(EXPERTS, dtype=jnp.int32) == expert
    results = []
    for layer_at in range(task_deltas.shape[1]):
        change = task_deltas[0, layer_at].astype(jnp.float32)
        magnitude = jnp.sum(jnp.abs(change), axis=0)
        group_total = magnitude
        for bit_at in range(groups.bit_length() - 1):
            group_total = group_total + swapped(group_total, SHARD, bit_at)
        grand_sum = one_axis_at_a_time(jnp.sum(magnitude), SHARD)
        rounded = lax.optimization_barrier(keep_probability(group_total, grand_sum, rows_whole))
        probability = rounded.astype(jnp.float32)
        own_limit = jnp.sum(jnp.where(selector, keep_limits[0, layer_at], 0))
        retained = jnp.where(
            rank_scores[0, layer_at] < own_limit, change / probability[None, :], jnp.float32(0.0)
        )
        portion = summed_on_arrival(retained, "task", 1)
        results.append(portion.astype(jnp.bfloat16))
    return jnp.stack(results)


def solution(mesh):
    finer = Mesh(
        mesh.devices.reshape(4, 4, 2, mesh.shape["task"]), ("shard_0", "shard_1", "shard_2", "task")
    )
    in_specs = (P("task", None, SHARD, None), P("task", None, SHARD, None), P("task", None, None))
    out_specs = P(None, SHARD, "task")
    return jax.shard_map(
        on_device, mesh=finer, in_specs=in_specs, out_specs=out_specs, check_vma=False
    )
```

profile of v0, /device:TPU:0, one launch (start us, length us, event | category | flops | bytes accessed | tf_op | source)
XLA Modules:
  0.0 136.6 jit_solution(17383141489137760862)
XLA Ops:
  0.0 3.3 %abs_reduce_fusion.6 = (f32[]{:T(128)}, f32[16384]{0:T(1024)S(1)}, f32[]{:T(128)}, f32[16384]{0:T(1024)S(1)}, f32[]{:T(128)}, /*index=5*/f32[16384]{0:T(1024)}, f32[]{:T(128)}, f32[16384]{0:T(1024)S(1)}) fusion(bf16[1,4,16,16384]{3,2,1,0:T(8,128)(2,1)} %param.3), kind=kLoop, calls=%fused_computation.18 | loop fusion | flops 4128764 | bytes 2359312 | tf_op jit(solution)/shard_map/reduce_sum | solution.py:54
  4.4 1.7 %slice_convert_fusion.3 = (f32[1,1,16,16384]{3,2,1,0:T(8,128)}, f32[1,1,16,16384]{3,2,1,0:T(8,128)}, f32[1,1,16,16384]{3,2,1,0:T(8,128)S(1)}, f32[1,1,16,16384]{3,2,1,0:T(8,128)}) fusion(bf16[1,4,16,16384]{3,2,1,0:T(8,128)(2,1)S(1)} %copy-done), kind=kLoop, calls=%fused_computation.24 | loop fusion | flops 1048576 | bytes 6291456 | tf_op jit(solution)/shard_map/convert_element_type | solution.py:49
  7.5 2.0 %collective-permute-start.7 = (f32[16384]{0:T(1024)}, f32[16384]{0:T(1024)}, u32[]{:S(2)}, u32[]{:S(2)}) collective-permute-start(f32[16384]{0:T(1024)} %add.108), channel_id=1, source_target_pairs={{0,8},{4,12},{8,0},{12,4},{16,24},{20,28},{24,16},{28,20},{32,40},... | collective-permute-start | bytes 196616 | tf_op jit(solution)/shard_map/ppermute | solution.py:15
  9.5 6.2 %slice_compare_fusion.3 = (pred[1,1,16,16384]{3,2,1,0:T(8,128)(4,1)}, pred[1,1,16,16384]{3,2,1,0:T(8,128)(4,1)S(1)}, pred[1,1,16,16384]{3,2,1,0:T(8,128)(4,1)S(1)}, pred[1,1,16,16384]{3,2,1,0:T(8,128)(4,1)}) fusion(s32[1,4,16,16384]{3,2,1,0:T(8,128)} %param.4, s32[]{:T(128)} %get-tuple-element.13, s32[]{:T(128)} %get-tuple-element.14, s32[]{:T(128)} %get-tuple-element.15, ...), kind=kLoop, calls=%fused_computation.7 | loop fusion | flops 1048576 | bytes 5242896 | tf_op jit(solution)/shard_map/lt | solution.py:59
  15.7 11.2 %all-reduce.1 = (f32[]{:T(128)}, f32[]{:T(128)}, f32[]{:T(128)}, f32[]{:T(128)}) all-reduce(f32[]{:T(128)} %get-tuple-element.5, f32[]{:T(128)} %get-tuple-element.7, f32[]{:T(128)} %get-tuple-element.9, f32[]{:T(128)} %get-tuple-element.11), channel_id=1, replica_groups=mesh['shard_0'=4,'shard_1'=4,'shard_2'=2,'task'=4] {'shard_0'}, use_global_device_ids=true, to_apply=%region_3.4 | all-reduce | flops 4 | bytes 32 | tf_op jit(solution)/shard_map/psum | solution.py:20
  26.9 10.9 %all-reduce = (f32[]{:T(128)}, f32[]{:T(128)}, f32[]{:T(128)}, f32[]{:T(128)}) all-reduce(f32[]{:T(128)} %get-tuple-element.21, f32[]{:T(128)} %get-tuple-element.22, f32[]{:T(128)} %get-tuple-element.23, f32[]{:T(128)} %get-tuple-element.24), channel_id=1, replica_groups=mesh['shard_0'=4,'shard_1'=4,'shard_2'=2,'task'=4] {'shard_1'}, use_global_device_ids=true, to_apply=%region_4.5 | all-reduce | flops 4 | bytes 32 | tf_op jit(solution)/shard_map/psum | solution.py:20
  37.9 3.2 %all-reduce.2 = (f32[]{:T(128)}, f32[]{:T(128)}, f32[]{:T(128)}, f32[]{:T(128)}) all-reduce(f32[]{:T(128)} %get-tuple-element.17, f32[]{:T(128)} %get-tuple-element.18, f32[]{:T(128)} %get-tuple-element.19, f32[]{:T(128)} %get-tuple-element.20), channel_id=1, replica_groups=mesh['shard_0'=4,'shard_1'=4,'shard_2'=2,'task'=4] {'shard_2'}, use_global_device_ids=true, to_apply=%region_5.6 | all-reduce | flops 4 | bytes 32 | tf_op jit(solution)/shard_map/psum | solution.py:20
  42.1 1.7 %reshape.102 = f32[16,4,4096]{2,1,0:T(4,128)} reshape(f32[1,1,16,16384]{3,2,1,0:T(8,128)S(1)} %get-tuple-element.35) | data formatting | bytes 2097152 | tf_op jit(solution)/shard_map/convert_element_type | solution.py:49
  43.8 2.1 %lt.48 = pred[16,4,4096]{2,1,0:T(4,128)(4,1)} reshape(pred[1,1,16,16384]{3,2,1,0:T(8,128)(4,1)} %get-tuple-element.32) | data formatting | bytes 524288 | tf_op jit(solution)/shard_map/lt | solution.py:59
  51.7 1.9 %reshape.96 = f32[16,4,4096]{2,1,0:T(4,128)S(1)} reshape(f32[1,1,16,16384]{3,2,1,0:T(8,128)} %get-tuple-element.33) | data formatting | bytes 2097152 | tf_op jit(solution)/shard_map/convert_element_type | solution.py:49
  57.6 1.6 %collective-permute-start.3 = (f32[16384]{0:T(1024)}, f32[16384]{0:T(1024)}, u32[]{:S(2)}, u32[]{:S(2)}) collective-permute-start(f32[16384]{0:T(1024)} %add.98), channel_id=1, source_target_pairs={{0,8},{4,12},{8,0},{12,4},{16,24},{20,28},{24,16},{28,20},{32,40},... | collective-permute-start | bytes 196616 | tf_op jit(solution)/shard_map/ppermute | solution.py:15
  62.8 1.8 %fusion.3 = f32[4,16,4096]{2,0,1:T(4,128)S(1)} fusion(pred[16,4,4096]{2,1,0:T(4,128)(4,1)} %lt.51, f32[16,4,4096]{2,1,0:T(4,128)} %reshape.102, f32[4,4096]{1,0:T(4,128)S(1)} %reshape.103), kind=kLoop, calls=%fused_computation.11 | loop fusion | flops 524288 | bytes 2424832 | tf_op jit(solution)/shard_map/transpose | solution.py:26
  64.6 1.6 %copy.7 = f32[4,16,4096]{2,1,0:T(8,128)} copy(f32[4,16,4096]{2,0,1:T(4,128)S(1)} %fusion.3) | data formatting | bytes 2097152 | tf_op jit(solution)/shard_map/transpose | solution.py:26
  66.3 4.5 %all-to-all-start.3 = ((f32[4,16,4096]{2,1,0:T(8,128)}), f32[4,16,4096]{2,1,0:T(8,128)}, u32[]{:S(2)}, u32[]{:S(2)}) async-start(f32[4,16,4096]{2,1,0:T(8,128)} %copy.7), calls=%async_computation.3 | async-start | bytes 2097152 | tf_op jit(solution)/shard_map/all_to_all | solution.py:31
  74.4 1.6 %copy.6 = f32[4,16,4096]{2,1,0:T(8,128)} copy(f32[4,16,4096]{2,0,1:T(4,128)S(1)} %fusion.2) | data formatting | bytes 2097152 | tf_op jit(solution)/shard_map/transpose | solution.py:26
  77.0 8.6 %all-to-all-done.3 = f32[4,16,4096]{2,1,0:T(8,128)} async-done(((f32[4,16,4096]{2,1,0:T(8,128)}), f32[4,16,4096]{2,1,0:T(8,128)}, u32[]{:S(2)}, u32[]{:S(2)}) %all-to-all-start.3) | async-done | bytes 1048608 | tf_op jit(solution)/shard_map/all_to_all | solution.py:31
  85.6 3.5 %all-to-all-start.2 = ((f32[4,16,4096]{2,1,0:T(8,128)}), f32[4,16,4096]{2,1,0:T(8,128)S(1)}, u32[]{:S(2)}, u32[]{:S(2)}) async-start(f32[4,16,4096]{2,1,0:T(8,128)} %copy.6), calls=%async_computation.2 | async-start | bytes 2097152 | tf_op jit(solution)/shard_map/all_to_all | solution.py:31
  90.5 1.6 %copy.5 = f32[4,16,4096]{2,1,0:T(8,128)} copy(f32[4,16,4096]{2,0,1:T(4,128)S(1)} %fusion.1) | data formatting | bytes 2097152 | tf_op jit(solution)/shard_map/transpose | solution.py:26
  93.1 9.9 %all-to-all-done.2 = f32[4,16,4096]{2,1,0:T(8,128)S(1)} async-done(((f32[4,16,4096]{2,1,0:T(8,128)}), f32[4,16,4096]{2,1,0:T(8,128)S(1)}, u32[]{:S(2)}, u32[]{:S(2)}) %all-to-all-start.2) | async-done | bytes 1048608 | tf_op jit(solution)/shard_map/all_to_all | solution.py:31
  103.0 4.3 %all-to-all-start.1 = ((f32[4,16,4096]{2,1,0:T(8,128)}), f32[4,16,4096]{2,1,0:T(8,128)}, u32[]{:S(2)}, u32[]{:S(2)}) async-start(f32[4,16,4096]{2,1,0:T(8,128)} %copy.5), calls=%async_computation.1 | async-start | bytes 2097152 | tf_op jit(solution)/shard_map/all_to_all | solution.py:31
  107.7 1.6 %copy.4 = f32[4,16,4096]{2,1,0:T(8,128)} copy(f32[4,16,4096]{2,0,1:T(4,128)S(1)} %fusion) | data formatting | bytes 2097152 | tf_op jit(solution)/shard_map/transpose | solution.py:26
  109.3 11.0 %all-to-all-done.1 = f32[4,16,4096]{2,1,0:T(8,128)} async-done(((f32[4,16,4096]{2,1,0:T(8,128)}), f32[4,16,4096]{2,1,0:T(8,128)}, u32[]{:S(2)}, u32[]{:S(2)}) %all-to-all-start.1) | async-done | bytes 1048608 | tf_op jit(solution)/shard_map/all_to_all | solution.py:31
  120.3 3.5 %all-to-all-start = ((f32[4,16,4096]{2,1,0:T(8,128)}), f32[4,16,4096]{2,1,0:T(8,128)S(1)}, u32[]{:S(2)}, u32[]{:S(2)}) async-start(f32[4,16,4096]{2,1,0:T(8,128)} %copy.4), calls=%async_computation | async-start | bytes 2097152 | tf_op jit(solution)/shard_map/all_to_all | solution.py:31
  126.5 9.2 %all-to-all-done = f32[4,16,4096]{2,1,0:T(8,128)S(1)} async-done(((f32[4,16,4096]{2,1,0:T(8,128)}), f32[4,16,4096]{2,1,0:T(8,128)S(1)}, u32[]{:S(2)}, u32[]{:S(2)}) %all-to-all-start) | async-done | bytes 1048608 | tf_op jit(solution)/shard_map/all_to_all | solution.py:31
  (48 shorter events, 25.2 us)
Async XLA Ops:
  0.0 4.4 %copy-start = (bf16[1,4,16,16384]{3,2,1,0:T(8,128)(2,1)S(1)}, bf16[1,4,16,16384]{3,2,1,0:T(8,128)(2,1)}, u32[]{:S(2)}) copy-start(bf16[1,4,16,16384]{3,2,1,0:T(8,128)(2,1)} %param.3) | copy-start | bytes 6291460
  3.3 3.5 %collective-permute-start.6 = (f32[16384]{0:T(1024)S(1)}, f32[16384]{0:T(1024)S(1)}, u32[]{:S(2)}, u32[]{:S(2)}) collective-permute-start(f32[16384]{0:T(1024)S(1)} %get-tuple-element.12), channel_id=1, source_target_pairs={{0,4},{4,0},{8,12},{12,8},{16,20},{20,16},{24,28},{28,24},{32,36},... | collective-permute-start | bytes 196616 | tf_op jit(solution)/shard_map/ppermute | solution.py:15
  3.3 50.9 %collective-permute-start.4 = (f32[16384]{0:T(1024)}, f32[16384]{0:T(1024)}, u32[]{:S(2)}, u32[]{:S(2)}) collective-permute-start(f32[16384]{0:T(1024)} %get-tuple-element.10), channel_id=1, source_target_pairs={{0,4},{4,0},{8,12},{12,8},{16,20},{20,16},{24,28},{28,24},{32,36},... | collective-permute-start | bytes 196616 | tf_op jit(solution)/shard_map/ppermute | solution.py:15
  3.9 52.3 %collective-permute-start.2 = (f32[16384]{0:T(1024)S(1)}, f32[16384]{0:T(1024)}, u32[]{:S(2)}, u32[]{:S(2)}) collective-permute-start(f32[16384]{0:T(1024)S(1)} %get-tuple-element.8), channel_id=1, source_target_pairs={{0,4},{4,0},{8,12},{12,8},{16,20},{20,16},{24,28},{28,24},{32,36},... | collective-permute-start | bytes 196616 | tf_op jit(solution)/shard_map/ppermute | solution.py:15
  3.9 55.4 %collective-permute-start = (f32[16384]{0:T(1024)S(1)}, f32[16384]{0:T(1024)}, u32[]{:S(2)}, u32[]{:S(2)}) collective-permute-start(f32[16384]{0:T(1024)S(1)} %get-tuple-element.6), channel_id=1, source_target_pairs={{0,4},{4,0},{8,12},{12,8},{16,20},{20,16},{24,28},{28,24},{32,36},... | collective-permute-start | bytes 196616 | tf_op jit(solution)/shard_map/ppermute | solution.py:15
  4.4 1.7 %copy-start.3 = (s32[1,4,8]{2,1,0:T(4,128)S(1)}, s32[1,4,8]{2,1,0:T(4,128)}, u32[]{:S(2)}) copy-start(s32[1,4,8]{2,1,0:T(4,128)} %param.5) | copy-start | bytes 388
  7.5 53.1 %collective-permute-start.7 = (f32[16384]{0:T(1024)}, f32[16384]{0:T(1024)}, u32[]{:S(2)}, u32[]{:S(2)}) collective-permute-start(f32[16384]{0:T(1024)} %add.108), channel_id=1, source_target_pairs={{0,8},{4,12},{8,0},{12,4},{16,24},{20,28},{24,16},{28,20},{32,40},... | collective-permute-start | bytes 196616 | tf_op jit(solution)/shard_map/ppermute | solution.py:15
  15.7 30.2 %copy-start.2 = (f32[1,1,16,16384]{3,2,1,0:T(8,128)S(1)}, f32[1,1,16,16384]{3,2,1,0:T(8,128)}, u32[]{:S(2)}) copy-start(f32[1,1,16,16384]{3,2,1,0:T(8,128)} %get-tuple-element.36) | copy-start | bytes 3145732
  43.8 5.2 %copy-start.1 = (f32[1,1,16,16384]{3,2,1,0:T(8,128)S(1)}, f32[1,1,16,16384]{3,2,1,0:T(8,128)}, u32[]{:S(2)}) copy-start(f32[1,1,16,16384]{3,2,1,0:T(8,128)} %get-tuple-element.34) | copy-start | bytes 3145732
  55.7 15.0 %collective-permute-start.5 = (f32[16384]{0:T(1024)}, f32[16384]{0:T(1024)}, u32[]{:S(2)}, u32[]{:S(2)}) collective-permute-start(f32[16384]{0:T(1024)} %add.103), channel_id=1, source_target_pairs={{0,8},{4,12},{8,0},{12,4},{16,24},{20,28},{24,16},{28,20},{32,40},... | collective-permute-start | bytes 196616 | tf_op jit(solution)/shard_map/ppermute | solution.py:15
  57.6 18.4 %collective-permute-start.3 = (f32[16384]{0:T(1024)}, f32[16384]{0:T(1024)}, u32[]{:S(2)}, u32[]{:S(2)}) collective-permute-start(f32[16384]{0:T(1024)} %add.98), channel_id=1, source_target_pairs={{0,8},{4,12},{8,0},{12,4},{16,24},{20,28},{24,16},{28,20},{32,40},... | collective-permute-start | bytes 196616 | tf_op jit(solution)/shard_map/ppermute | solution.py:15
  60.1 32.1 %collective-permute-start.1 = (f32[16384]{0:T(1024)S(1)}, f32[16384]{0:T(1024)}, u32[]{:S(2)}, u32[]{:S(2)}) collective-permute-start(f32[16384]{0:T(1024)S(1)} %add.93), channel_id=1, source_target_pairs={{0,8},{4,12},{8,0},{12,4},{16,24},{20,28},{24,16},{28,20},{32,40},... | collective-permute-start | bytes 196616 | tf_op jit(solution)/shard_map/ppermute | solution.py:15
  66.3 19.3 %all-to-all-start.3 = ((f32[4,16,4096]{2,1,0:T(8,128)}), f32[4,16,4096]{2,1,0:T(8,128)}, u32[]{:S(2)}, u32[]{:S(2)}) async-start(f32[4,16,4096]{2,1,0:T(8,128)} %copy.7), calls=%async_computation.3 | async-start | bytes 2097152 | tf_op jit(solution)/shard_map/all_to_all | solution.py:31
  85.6 17.4 %all-to-all-start.2 = ((f32[4,16,4096]{2,1,0:T(8,128)}), f32[4,16,4096]{2,1,0:T(8,128)S(1)}, u32[]{:S(2)}, u32[]{:S(2)}) async-start(f32[4,16,4096]{2,1,0:T(8,128)} %copy.6), calls=%async_computation.2 | async-start | bytes 2097152 | tf_op jit(solution)/shard_map/all_to_all | solution.py:31
  103.0 17.4 %all-to-all-start.1 = ((f32[4,16,4096]{2,1,0:T(8,128)}), f32[4,16,4096]{2,1,0:T(8,128)}, u32[]{:S(2)}, u32[]{:S(2)}) async-start(f32[4,16,4096]{2,1,0:T(8,128)} %copy.5), calls=%async_computation.1 | async-start | bytes 2097152 | tf_op jit(solution)/shard_map/all_to_all | solution.py:31
  120.3 15.4 %all-to-all-start = ((f32[4,16,4096]{2,1,0:T(8,128)}), f32[4,16,4096]{2,1,0:T(8,128)S(1)}, u32[]{:S(2)}, u32[]{:S(2)}) async-start(f32[4,16,4096]{2,1,0:T(8,128)} %copy.4), calls=%async_computation | async-start | bytes 2097152 | tf_op jit(solution)/shard_map/all_to_all | solution.py:31
where the time goes:
time: 138 us; the launch traced here: 137 us
  waiting for transfers between devices  38.7 us (28%)
  other arithmetic  29.8 us (22%)
  blocking collectives  25.3 us (18%)
  starting transfers between devices  21.3 us (15%)
  local copies, waits for them, and re-layouts  18.8 us (14%)
  between operations  2.66 us (2%)
    all_to_all x4, waiting for transfers between devices, summed_on_arrival(): lax.all_to_all(tiles, axis, split_axis=0, concat_axis=0, tiled=True)  38.7 us
    psum x3, blocking collectives, one_axis_at_a_time(): value = lax.psum(value, axis)  25.3 us
    all_to_all x4, starting transfers between devices, summed_on_arrival(): lax.all_to_all(tiles, axis, split_axis=0, concat_axis=0, tiled=True)  15.8 us
    transpose x4, local copies, waits for them, and re-layouts, split_up(): return jnp.moveaxis(value.reshape(*before, size, -1, *after), dim, 0)  6.48 us
    lt x1, other arithmetic, on_device(): rank_scores[0, layer_at] < own_limit  6.18 us
    lt x4, local copies, waits for them, and re-layouts, on_device(): rank_scores[0, layer_at] < own_limit  5.6 us
    ppermute x8, starting transfers between devices, swapped(): return lax.ppermute(value, axis, pairs)  5.56 us
    transpose x4, other arithmetic, split_up(): return jnp.moveaxis(value.reshape(*before, size, -1, *after), dim, 0)  5.06 us
  transfers between devices with their start and end apart: 12, of which 4 were waited for; matrix products, arithmetic and copies ran while one was open for 32% of the time, Pallas kernels for 0%

commit v1 on v0

v1 whole, which is shorter than its diff:
```python
import functools

import jax
import jax.numpy as jnp
from jax import lax
from jax.experimental import pallas as pl
from jax.experimental.pallas import tpu as pltpu
from jax.sharding import PartitionSpec as P

EXPERTS = 8
ROWS = 64
FF = 16384
LAYERS = 4
TASKS = 4
SHARDS = 32
GROUP = 4
PLANE = 8
HERE = 16
HALF = 2048
LANES = 128
PARTS = HALF // LANES
RAW = 4

MESH = pl.DeviceIdType.MESH
F32 = jnp.float32
BF16 = jnp.bfloat16


def kernel(
    delta, score, limit, out,
    dbuf, sbuf, masked, sums, sums_in, prob, prob_in, inv, acc, raw_in,
    tot, tot_x, tot2, tot_z,
    sem_d, sem_s, sem_sum, sem_x, sem_z, sem_p, sem_py, sem_r, sem_o,
):
    s, t = lax.axis_index("shard"), lax.axis_index("task")
    expert = lax.div(s, GROUP)
    member = lax.rem(s, GROUP)
    first = expert * GROUP
    plane, spot = lax.div(s, PLANE) * PLANE, lax.rem(s, PLANE)

    def at_task(d):
        return (s, lax.rem(t + d, TASKS))

    def at_x(d):
        return (lax.rem(s + PLANE * d, SHARDS), t)

    def at_plane(d):
        return (plane + lax.rem(spot + d, PLANE), t)

    def at_group(d):
        return (first + lax.rem(member + d, GROUP), t)

    def send(src, dst, sems, at, to):
        copy = pltpu.make_async_remote_copy(
            src_ref=src, dst_ref=dst, send_sem=sems.at[(0, *at)], recv_sem=sems.at[(1, *at)],
            device_id=to, device_id_type=MESH,
        )
        copy.start()
        return copy

    load_d = [pltpu.make_async_copy(delta.at[0, l], dbuf.at[l], sem_d.at[l]) for l in range(LAYERS)]
    load_s = [pltpu.make_async_copy(score.at[0, l], sbuf.at[l], sem_s.at[l]) for l in range(LAYERS)]
    load_d[0].start()
    load_s[0].start()
    for l in range(1, LAYERS):
        load_d[l].start()
    for l in range(1, LAYERS):
        load_s[l].start()

    barrier = pltpu.get_barrier_semaphore()
    peers = [at_task(d) for d in (1, 2, 3)] + [at_x(d) for d in (1, 2, 3)] + [at_plane(d) for d in range(1, PLANE)]
    for peer in peers:
        pl.semaphore_signal(barrier, inc=1, device_id=peer, device_id_type=MESH)

    def sum_layer(l):
        def body(i, carry):
            b, h = lax.div(i, 2), lax.rem(i, 2)
            for j in range(PARTS):
                cols = pl.ds(pl.multiple_of(i * HALF + j * LANES, LANES), LANES)
                change = jnp.abs(dbuf[l, :, cols].astype(F32))
                sums[b, l, h, j : j + 1, :] = jnp.sum(change, axis=0, keepdims=True)
            return carry

        lax.fori_loop(0, 2 * TASKS, body, 0)

    def mask_layer(l):
        own_limit = limit[0, l, expert]

        def body(i, carry):
            b, h = lax.div(i, 2), lax.rem(i, 2)
            for j in range(PARTS):
                cols = pl.ds(pl.multiple_of(i * HALF + j * LANES, LANES), LANES)
                keep = sbuf[l, :, cols] < own_limit
                masked[b, l, h, :, j * LANES : (j + 1) * LANES] = jnp.where(
                    keep, dbuf[l, :, cols].astype(F32), F32(0.0)
                ).astype(BF16)
            return carry

        lax.fori_loop(0, 2 * TASKS, body, 0)

    copies = []

    def send_raw(l):
        for d in (1, 3, 2):
            owner = lax.rem(t + d, TASKS)
            copies.append((("raw", d, l), send(masked.at[owner, l], raw_in.at[d - 1, l], sem_r, (d - 1, l), at_task(d))))

    load_d[0].wait()
    load_s[0].wait()
    mask_layer(0)
    pl.semaphore_wait(barrier, len(peers))
    send_raw(0)
    sum_layer(0)
    for l in range(1, LAYERS):
        load_d[l].wait()
        sum_layer(l)

    for d in range(1, GROUP):
        other = lax.rem(member + d, GROUP)
        copies.append((("sum", d), send(sums.at[other], sums_in.at[d - 1], sem_sum, (d - 1,), at_group(d))))
    for l in range(LAYERS):
        whole = sums[0, l, 0] + sums[0, l, 1]
        for b in range(1, TASKS):
            whole = whole + sums[b, l, 0] + sums[b, l, 1]
        tot[l : l + 1, :] = jnp.sum(whole, axis=0, keepdims=True)
    tot[LAYERS:, :] = jnp.zeros((8 - LAYERS, LANES), F32)
    for d in (1, 2, 3):
        copies.append((("x", d), send(tot, tot_x.at[d - 1], sem_x, (d - 1,), at_x(d))))

    for l in range(1, LAYERS):
        load_s[l].wait()
        mask_layer(l)
        send_raw(l)

    flight = dict(copies)
    for d in (1, 2, 3):
        flight["x", d].wait_recv()
    tot2[...] = tot[...] + tot_x[0] + tot_x[1] + tot_x[2]
    for d in range(1, PLANE):
        flight["z", d] = send(tot2, tot_z.at[d - 1], sem_z, (d - 1,), at_plane(d))
    for d in range(1, GROUP):
        flight["sum", d].wait_recv()
    for d in range(1, PLANE):
        flight["z", d].wait_recv()
    grand = tot2[...]
    for d in range(1, PLANE):
        grand = grand + tot_z[d - 1]
    grand_mean = jnp.sum(grand, axis=1, keepdims=True) / F32(EXPERTS * ROWS * FF)

    for l in range(LAYERS):
        mean_l = jnp.broadcast_to(grand_mean[l : l + 1, :], (PARTS, LANES))
        for h in range(2):
            column = sums[member, l, h] + sums_in[0, l, h] + sums_in[1, l, h] + sums_in[2, l, h]
            column = column / F32(ROWS)
            prob[member, l, h] = (0.2 + 0.7 * column / (column + mean_l)).astype(BF16)
    for d in range(1, GROUP):
        flight["p", d] = send(prob.at[member], prob.at[member], sem_p, (d - 1,), at_group(d))
    for d in range(1, GROUP):
        flight["p", d].wait_recv()
    for d in (1, 3, 2):
        owner = lax.rem(t + d, TASKS)
        flight["py", d] = send(prob.at[owner], prob_in.at[d - 1], sem_py, (d - 1,), at_task(d))

    def rescaled(block, tile, j):
        return block[:, j * LANES : (j + 1) * LANES].astype(F32) * tile[j : j + 1, :]

    for l in range(LAYERS):
        for h in range(2):
            tile = 1.0 / prob[t, l, h].astype(F32)
            block = masked.at[t, l, h]
            for j in range(PARTS):
                acc[l, h, :, j * LANES : (j + 1) * LANES] = rescaled(block, tile, j)
    for d in (1, 3, 2):
        flight["py", d].wait_recv()
    for d in (1, 2, 3):
        for l in range(LAYERS):
            for h in range(2):
                inv[d - 1, l, h] = 1.0 / prob_in[d - 1, l, h].astype(F32)
    store = []
    for l in range(LAYERS):
        for d in (1, 3, 2):
            flight["raw", d, l].wait_recv()
        for h in range(2):
            tiles = [inv[d, l, h] for d in range(3)]
            for j in range(PARTS):
                here = acc[l, h, :, j * LANES : (j + 1) * LANES]
                for d in range(3):
                    here = here + rescaled(raw_in.at[d, l, h], tiles[d], j)
                out[l, :, h * HALF + j * LANES : h * HALF + (j + 1) * LANES] = here.astype(BF16)
    for copy in flight.values():
        copy.wait_send()


def on_device(task_deltas, rank_scores, keep_limits):
    dma = pltpu.SemaphoreType.DMA
    return pl.pallas_call(
        kernel,
        out_shape=jax.ShapeDtypeStruct((LAYERS, HERE, 2 * HALF), BF16),
        in_specs=[
            pl.BlockSpec(memory_space=pl.ANY),
            pl.BlockSpec(memory_space=pl.ANY),
            pl.BlockSpec(memory_space=pltpu.SMEM),
        ],
        out_specs=pl.BlockSpec(memory_space=pltpu.VMEM),
        scratch_shapes=[
            pltpu.VMEM((LAYERS, HERE, FF), BF16),
            pltpu.VMEM((LAYERS, HERE, FF), jnp.int32),
            pltpu.VMEM((TASKS, LAYERS, 2, HERE, HALF), BF16),
            pltpu.VMEM((TASKS, LAYERS, 2, PARTS, LANES), F32),
            pltpu.VMEM((3, LAYERS, 2, PARTS, LANES), F32),
            pltpu.VMEM((TASKS, LAYERS, 2, PARTS, LANES), BF16),
            pltpu.VMEM((3, LAYERS, 2, PARTS, LANES), BF16),
            pltpu.VMEM((3, LAYERS, 2, PARTS, LANES), F32),
            pltpu.VMEM((LAYERS, 2, HERE, HALF), F32),
            pltpu.VMEM((3, LAYERS, 2, HERE, HALF), BF16),
            pltpu.VMEM((8, LANES), F32),
            pltpu.VMEM((3, 8, LANES), F32),
            pltpu.VMEM((8, LANES), F32),
            pltpu.VMEM((PLANE - 1, 8, LANES), F32),
            dma((LAYERS,)),
            dma((LAYERS,)),
            dma((2, 3)),
            dma((2, 3)),
            dma((2, PLANE - 1)),
            dma((2, 3)),
            dma((2, 3)),
            dma((2, 3, LAYERS)),
            dma((LAYERS,)),
        ],
        compiler_params=pltpu.CompilerParams(collective_id=0, has_side_effects=True),
    )(task_deltas, rank_scores, keep_limits)


def solution(mesh):
    in_specs = (P("task", None, "shard", None), P("task", None, "shard", None), P("task", None, None))
    return jax.shard_map(on_device, mesh=mesh, in_specs=in_specs, out_specs=P(None, "shard", "task"), check_vma=False)
```

time: 138 us -> 37.3 us (0.27)
  waiting for transfers between devices: 38.7 us -> 0 us
  Pallas kernels: 0 us -> 35.1 us
  other arithmetic: 29.8 us -> 0 us
  blocking collectives: 25.3 us -> 0 us
  starting transfers between devices: 21.3 us -> 0 us
  local copies, waits for them, and re-layouts: 18.8 us -> 1.87 us
  between operations: 2.66 us -> 0.01 us
    all_to_all x4 -> x0, waiting for transfers between devices: 38.7 us -> none  [summed_on_arrival(): lax.all_to_all(tiles, axis, split_axis=0, concat_axis=0, tiled=True)]
    pallas_call x0 -> x1, Pallas kernels: none -> 35.1 us  [on_device(): pl.pallas_call(kernel, out_shape=jax.ShapeDtypeStruct((LAYERS, HERE, 2 *...]
    psum x3 -> x0, blocking collectives: 25.3 us -> none  [one_axis_at_a_time(): value = lax.psum(value, axis)]
    all_to_all x4 -> x0, starting transfers between devices: 15.8 us -> none  [summed_on_arrival(): lax.all_to_all(tiles, axis, split_axis=0, concat_axis=0, tiled=True)]
    reduce_sum x6 -> x0, other arithmetic: 6.78 us -> none  [the longest x1 3.34 us: on_device(): grand_sum = one_axis_at_a_time(jnp.sum(magnitude), SHARD)]
    transpose x4 -> x0, local copies, waits for them, and re-layouts: 6.48 us -> none  [split_up(): return jnp.moveaxis(value.reshape(*before, size, -1, *after), dim, 0)]
    convert_element_type x5 -> x0, other arithmetic: 6.48 us -> none  [the longest x4 4.75 us: keep_probability(): (0.2 + 0.7 * column_mean / (column_mean + grand_mean)).astype(jnp.bfloat16)]
    lt x1 -> x0, other arithmetic: 6.18 us -> none  [on_device(): rank_scores[0, layer_at] < own_limit]
  transfers between devices with their start and end apart: 12 -> 0, of which waited for: 4 -> 0; matrix products, arithmetic and copies ran while one was open for 32% -> 0% of each run, Pallas kernels for 0% -> 0%
where the time goes in v1:
time: 37.3 us; the launch traced here: 37 us
  Pallas kernels  35.1 us (94%)
  local copies, waits for them, and re-layouts  1.87 us (5%)
    pallas_call x1, Pallas kernels, on_device(): pl.pallas_call(kernel, out_shape=jax.ShapeDtypeStruct((LAYERS, HERE, 2 *...  35.1 us
    unnamed x1, local copies, waits for them, and re-layouts  1.87 us

profile of v1, /device:TPU:0, one launch (start us, length us, event | category | flops | bytes accessed | tf_op | source)
XLA Modules:
  0.0 37.0 jit_solution(12023721967182266368)
XLA Ops:
  0.0 35.1 %shard_map.37 = bf16[4,16,4096]{2,1,0:T(8,128)(2,1)} custom-call(bf16[1,4,16,16384]{3,2,1,0:T(8,128)(2,1)} %delta.1, s32[1,4,16,16384]{3,2,1,0:T(8,128)} %score.1, s32[1,4,8]{2,1,0:T(4,128)} %limit.1), custom_call_target="tpu_custom_call" | custom-call | tf_op jit(solution)/shard_map/pallas_call | solution.py:196
  35.1 1.9 %copy.5 = bf16[4,16,4096]{2,1,0:T(8,128)(2,1)} copy(bf16[4,16,4096]{2,1,0:T(8,128)(2,1)} %shard_map.37) | data formatting | bytes 1048576

commit v2 on v1

v2 whole, which is shorter than its diff:
```python
import functools

import jax
import jax.numpy as jnp
from jax import lax
from jax.experimental import pallas as pl
from jax.experimental.pallas import tpu as pltpu
from jax.sharding import PartitionSpec as P

EXPERTS = 8
ROWS = 64
FF = 16384
LAYERS = 4
TASKS = 4
SHARDS = 32
GROUP = 4
HERE = 16
HALF = 2048
LANES = 128
PARTS = HALF // LANES
RAW = 2
REST = LAYERS - RAW

MESH = pl.DeviceIdType.MESH
F32 = jnp.float32
BF16 = jnp.bfloat16


def kernel(
    delta, score, limit_in, out,
    limit, dbuf, sbuf, masked, sums, sums_in, prob, prob_in, inv, acc, raw_in,
    far, far_in, joint, joint_in, tot, tot_z, tot2, tot_x, grand,
    sem_load, sem_sent, sem_got, sem_f, sem_j,
):
    s, t = lax.axis_index("shard"), lax.axis_index("task")
    expert = lax.div(s, GROUP)
    member = lax.rem(s, GROUP)
    first = expert * GROUP
    late = lax.rem(expert, 2)
    hub = (expert - late) * GROUP
    other = hub + (1 - late) * GROUP

    def at_task(d):
        return (s, lax.rem(t + d, TASKS))

    def at_x(d):
        return (lax.rem(s + 2 * GROUP * d, SHARDS), t)

    def at_group(d):
        return (first + lax.rem(member + d, GROUP), t)

    def send(src, dst, kind, to, got=None):
        copy = pltpu.make_async_remote_copy(
            src_ref=src, dst_ref=dst, send_sem=sem_sent.at[kind], recv_sem=sem_got.at[kind] if got is None else got,
            device_id=to, device_id_type=MESH,
        )
        copy.start()
        return copy

    def wait(ref, sem):
        pltpu.make_async_copy(ref, ref, sem).wait()

    def shares(ref):
        return {0: ref.at[pl.ds(0, 1)], 1: ref.at[:, pl.ds(0, 2)], 2: ref.at[pl.ds(0, 2)], 4: ref}[RAW]

    SUM, TOTAL, TOTAL_X, GRAND, PROB, PROB_Y, ENTRY, FAR, JOINT = range(9)

    barrier = pltpu.get_barrier_semaphore()

    def greet(to):
        pl.semaphore_signal(barrier, inc=1, device_id=to, device_id_type=MESH)

    for d in (1, 2, 3):
        greet(at_task(d))
        greet(at_group(d))

    @pl.when(late == 0)
    def _():
        for d in (1, 2, 3):
            greet(at_x(d))
        for m in range(GROUP):
            greet((other + m, t))

    loads = [
        pltpu.make_async_copy(limit_in, limit, sem_load.at[0]),
        pltpu.make_async_copy(delta.at[0, 0], dbuf.at[0], sem_load.at[1]),
        pltpu.make_async_copy(score.at[0, 0], sbuf.at[0], sem_load.at[2]),
        pltpu.make_async_copy(delta.at[0, pl.ds(1, LAYERS - 1)], dbuf.at[pl.ds(1, LAYERS - 1)], sem_load.at[3]),
        pltpu.make_async_copy(score.at[0, pl.ds(1, LAYERS - 1)], sbuf.at[pl.ds(1, LAYERS - 1)], sem_load.at[4]),
    ]
    for load in loads:
        load.start()

    def sum_layer(l):
        def body(i, carry):
            b, h = lax.div(i, 2), lax.rem(i, 2)
            for j in range(PARTS):
                cols = pl.ds(pl.multiple_of(i * HALF + j * LANES, LANES), LANES)
                change = jnp.abs(dbuf[l, :, cols].astype(F32))
                sums[b, l, h, j : j + 1, :] = jnp.sum(change, axis=0, keepdims=True)
            return carry

        lax.fori_loop(0, 2 * TASKS, body, 0)

    def mask_layer(l):
        own_limit = limit[0, l, expert]

        def body(i, carry):
            b, h = lax.div(i, 2), lax.rem(i, 2)
            for j in range(PARTS):
                cols = pl.ds(pl.multiple_of(i * HALF + j * LANES, LANES), LANES)
                keep = sbuf[l, :, cols] < own_limit
                masked[b, l, h, :, j * LANES : (j + 1) * LANES] = jnp.where(
                    keep, dbuf[l, :, cols].astype(F32), F32(0.0)
                ).astype(BF16)
            return carry

        lax.fori_loop(0, 2 * TASKS, body, 0)

    flight = []

    def send_raw(l):
        for d in (1, 3, 2) if l < RAW else (1, 3):
            owner = lax.rem(t + d, TASKS)
            if l < RAW:
                flight.append(send(masked.at[owner, l], raw_in.at[d - 1, l], ENTRY, at_task(d)))
            else:
                h = 1 if d == 1 else 0
                flight.append(send(masked.at[owner, l, h], raw_in.at[d - 1, l, h], ENTRY, at_task(d)))

    with jax.named_scope("load"):
        for load in loads[:3]:
            load.wait()
    with jax.named_scope("mask0"):
        mask_layer(0)
    with jax.named_scope("bar"):
        pl.semaphore_wait(barrier, 9 + late)
    send_raw(0)
    with jax.named_scope("sums"):
        sum_layer(0)
        loads[3].wait()
        for l in range(1, LAYERS):
            sum_layer(l)

    for l in range(LAYERS):
        whole = sums[0, l, 0] + sums[0, l, 1]
        for b in range(1, TASKS):
            whole = whole + sums[b, l, 0] + sums[b, l, 1]
        tot[l : l + 1, :] = jnp.sum(whole, axis=0, keepdims=True)
    tot[LAYERS:, :] = jnp.zeros((8 - LAYERS, LANES), F32)

    @pl.when(late == 0)
    def _():
        for d in range(1, GROUP):
            send(tot, tot_z.at[d - 1], TOTAL, at_group(d))

    @pl.when(late == 1)
    def _():
        for m in range(GROUP):
            send(tot, tot_z.at[GROUP - 1 + member], TOTAL, (other + m, t))

    for d in range(1, GROUP):
        send(sums.at[lax.rem(member + d, GROUP)], sums_in.at[d - 1], SUM, at_group(d))

    with jax.named_scope("masks"):
        loads[4].wait()
        for l in range(1, LAYERS):
            mask_layer(l)
            send_raw(l)

    with jax.named_scope("totals"):

        @pl.when(late == 0)
        def _():
            wait(tot_z, sem_got.at[TOTAL])
            whole = tot[...]
            for d in range(2 * GROUP - 1):
                whole = whole + tot_z[d]
            tot2[...] = whole
            for d in (1, 2, 3):
                send(tot2, tot_x.at[d - 1], TOTAL_X, at_x(d))
            wait(tot_x, sem_got.at[TOTAL_X])
            grand[...] = tot2[...] + tot_x[0] + tot_x[1] + tot_x[2]
            send(grand, grand, GRAND, (other + member, t))

        @pl.when(late == 1)
        def _():
            wait(grand, sem_got.at[GRAND])

    grand_mean = jnp.sum(grand[...], axis=1, keepdims=True) / F32(EXPERTS * ROWS * FF)
    with jax.named_scope("waitsum"):
        wait(sums_in, sem_got.at[SUM])

    for l in range(LAYERS):
        mean_l = jnp.broadcast_to(grand_mean[l : l + 1, :], (PARTS, LANES))
        for h in range(2):
            column = sums[member, l, h] + sums_in[0, l, h] + sums_in[1, l, h] + sums_in[2, l, h]
            column = column / F32(ROWS)
            prob[member, l, h] = (0.2 + 0.7 * column / (column + mean_l)).astype(BF16)
    for d in range(1, GROUP):
        send(prob.at[member], prob.at[member], PROB, at_group(d))
    with jax.named_scope("waitp"):
        wait(prob.at[pl.ds(0, GROUP - 1)], sem_got.at[PROB])

    def rescaled(block, tile, j):
        return block[:, j * LANES : (j + 1) * LANES].astype(F32) * tile[j : j + 1, :]

    far_owner = lax.rem(t + 2, TASKS)
    with jax.named_scope("far"):
        for l in range(RAW, LAYERS):
            for h in range(2):
                tile = 1.0 / prob[far_owner, l, h].astype(F32)
                for j in range(PARTS):
                    far[h, l - RAW, :, j * LANES : (j + 1) * LANES] = rescaled(
                        masked.at[far_owner, l, h], tile, j
                    ).astype(BF16)
                flight.append(
                    send(far.at[h, l - RAW], far_in.at[h, l - RAW], FAR, at_task(3 if h else 1), sem_f.at[h, l - RAW])
                )
    for d in (1, 3):
        owner, h = lax.rem(t + d, TASKS), 1 if d == 1 else 0
        if RAW < LAYERS:
            rest = pl.ds(RAW, LAYERS - RAW)
            send(prob.at[owner, rest, h], prob_in.at[d - 1, rest, h], PROB_Y, at_task(d))
    for d in (1, 3, 2) if RAW else ():
        some = pl.ds(0, RAW)
        send(prob.at[lax.rem(t + d, TASKS), some], prob_in.at[d - 1, some], PROB_Y, at_task(d))

    with jax.named_scope("own"):
        for l in range(LAYERS):
            for h in range(2):
                tile = 1.0 / prob[t, l, h].astype(F32)
                for j in range(PARTS):
                    acc[l, h, :, j * LANES : (j + 1) * LANES] = rescaled(masked.at[t, l, h], tile, j)

    for l in range(RAW, LAYERS):
        for h in range(2):
            with jax.named_scope(f"waitfar#l={l}#h={h}"):
                wait(far_in.at[h, l - RAW], sem_f.at[h, l - RAW])
            owner = lax.rem(t + (3 if h else 1), TASKS)
            tile = 1.0 / prob[owner, l, h].astype(F32)
            for j in range(PARTS):
                cols = slice(j * LANES, (j + 1) * LANES)
                joint[h, l - RAW, :, cols] = (
                    rescaled(masked.at[owner, l, h], tile, j) + far_in[h, l - RAW, :, cols].astype(F32)
                ).astype(BF16)
            send(joint.at[h, l - RAW], joint_in.at[h, l - RAW], JOINT, at_task(3 if h else 1), sem_j.at[h, l - RAW])

    with jax.named_scope("waitpy"):
        wait(shares(prob_in), sem_got.at[PROB_Y])
    for d in (1, 2, 3):
        for l in range(LAYERS):
            for h in range(2):
                if l < RAW or (d, h) in ((1, 1), (3, 0)):
                    inv[d - 1, l, h] = 1.0 / prob_in[d - 1, l, h].astype(F32)
    with jax.named_scope("waitraw"):
        wait(shares(raw_in), sem_got.at[ENTRY])
    with jax.named_scope("raw"):
        for l in range(LAYERS):
            for h in range(2):
                sources = (1, 2, 3) if l < RAW else (1,) if h else (3,)
                tiles = {d: inv[d - 1, l, h] for d in sources}
                for j in range(PARTS):
                    cols = slice(j * LANES, (j + 1) * LANES)
                    here = acc[l, h, :, cols]
                    for d in sources:
                        here = here + rescaled(raw_in.at[d - 1, l, h], tiles[d], j)
                    if l < RAW:
                        out[l, :, h * HALF + j * LANES : h * HALF + (j + 1) * LANES] = here.astype(BF16)
                    else:
                        acc[l, h, :, cols] = here
    for l in range(RAW, LAYERS):
        for h in range(2):
            with jax.named_scope(f"waitjoint#l={l}#h={h}"):
                wait(joint_in.at[h, l - RAW], sem_j.at[h, l - RAW])
            for j in range(PARTS):
                cols = slice(j * LANES, (j + 1) * LANES)
                out[l, :, h * HALF + j * LANES : h * HALF + (j + 1) * LANES] = (
                    acc[l, h, :, cols] + joint_in[h, l - RAW, :, cols].astype(F32)
                ).astype(BF16)

    with jax.named_scope("waitsend"):

        @pl.when(late == 0)
        def _():
            wait(tot_z.at[pl.ds(0, GROUP - 1)], sem_sent.at[TOTAL])
            wait(tot_x, sem_sent.at[TOTAL_X])
            wait(grand, sem_sent.at[GRAND])

        @pl.when(late == 1)
        def _():
            wait(tot_z.at[pl.ds(0, GROUP)], sem_sent.at[TOTAL])

        wait(sums_in, sem_sent.at[SUM])
        wait(prob.at[pl.ds(0, GROUP - 1)], sem_sent.at[PROB])
        wait(shares(prob_in), sem_sent.at[PROB_Y])
        wait(shares(raw_in), sem_sent.at[ENTRY])
        if RAW < LAYERS:
            wait(far, sem_sent.at[FAR])
            wait(joint, sem_sent.at[JOINT])


def on_device(task_deltas, rank_scores, keep_limits):
    dma = pltpu.SemaphoreType.DMA
    inputs = (pltpu.with_memory_space_constraint(x, pltpu.HBM) for x in (task_deltas, rank_scores, keep_limits))
    return pl.pallas_call(
        kernel,
        out_shape=jax.ShapeDtypeStruct((LAYERS, HERE, 2 * HALF), BF16),
        in_specs=[pl.BlockSpec(memory_space=pl.ANY)] * 3,
        out_specs=pl.BlockSpec(memory_space=pltpu.VMEM),
        scratch_shapes=[
            pltpu.SMEM((1, LAYERS, EXPERTS), jnp.int32),
            pltpu.VMEM((LAYERS, HERE, FF), BF16),
            pltpu.VMEM((LAYERS, HERE, FF), jnp.int32),
            pltpu.VMEM((TASKS, LAYERS, 2, HERE, HALF), BF16),
            pltpu.VMEM((TASKS, LAYERS, 2, PARTS, LANES), F32),
            pltpu.VMEM((GROUP - 1, LAYERS, 2, PARTS, LANES), F32),
            pltpu.VMEM((TASKS, LAYERS, 2, PARTS, LANES), BF16),
            pltpu.VMEM((3, LAYERS, 2, PARTS, LANES), BF16),
            pltpu.VMEM((3, LAYERS, 2, PARTS, LANES), F32),
            pltpu.VMEM((LAYERS, 2, HERE, HALF), F32),
            pltpu.VMEM((3, LAYERS, 2, HERE, HALF), BF16),
            *[pltpu.VMEM((2, REST, HERE, HALF), BF16)] * 4,
            pltpu.VMEM((8, LANES), F32),
            pltpu.VMEM((2 * GROUP - 1, 8, LANES), F32),
            pltpu.VMEM((8, LANES), F32),
            pltpu.VMEM((3, 8, LANES), F32),
            pltpu.VMEM((8, LANES), F32),
            dma((5,)),
            dma((9,)),
            dma((7,)),
            dma((2, REST)),
            dma((2, REST)),
        ],
        compiler_params=pltpu.CompilerParams(
            collective_id=0, has_side_effects=True, vmem_limit_bytes=32 * 1024 * 1024
        ),
    )(*inputs)


def solution(mesh):
    in_specs = (P("task", None, "shard", None), P("task", None, "shard", None), P("task", None, None))
    return jax.shard_map(on_device, mesh=mesh, in_specs=in_specs, out_specs=P(None, "shard", "task"), check_vma=False)
```

time: 37.3 us -> 29.8 us (0.80)
  the two profiles are of different devices: /device:TPU:0 before, /device:TPU:64 now
where the time goes in v2:
time: 29.8 us; the launch traced here: 29.7 us
  Pallas kernels  28.9 us (97%)
  local copies, waits for them, and re-layouts  0.8 us (3%)
    pallas_call x1, Pallas kernels, on_device(): pl.pallas_call(kernel, out_shape=jax.ShapeDtypeStruct((LAYERS, HERE, 2 *...  28.9 us
    unnamed x1, local copies, waits for them, and re-layouts  0.8 us

profile of v2, /device:TPU:64, one launch (start us, length us, event | category | flops | bytes accessed | tf_op | source)
XLA Modules:
  0.0 29.7 jit_solution(17752355484662331622)
XLA Ops:
  0.0 28.9 %shard_map.37 = bf16[4,16,4096]{2,1,0:T(8,128)(2,1)S(1)} custom-call(bf16[1,4,16,16384]{3,2,1,0:T(8,128)(2,1)} %delta.1, s32[1,4,16,16384]{3,2,1,0:T(8,128)} %score.1, s32[1,4,8]{2,1,0:T(4,128)} %limit_in.1), custom_call_target="tpu_custom_call" | custom-call | tf_op jit(solution)/shard_map/pallas_call | solution.py:306
  28.9 0.8 %copy.5 = bf16[4,16,4096]{2,1,0:T(8,128)(2,1)} copy(bf16[4,16,4096]{2,1,0:T(8,128)(2,1)S(1)} %shard_map.37) | data formatting | bytes 1048576

commit v3 on v2

--- a/solution.py
+++ b/solution.py
@@ -18,7 +18,7 @@
 HALF = 2048
 LANES = 128
 PARTS = HALF // LANES
-RAW = 2
+RAW = 1
 REST = LAYERS - RAW
 
 MESH = pl.DeviceIdType.MESH
@@ -28,13 +28,14 @@
 
 def kernel(
     delta, score, limit_in, out,
-    limit, dbuf, sbuf, masked, sums, sums_in, prob, prob_in, inv, acc, raw_in,
+    limit, dbuf, sbuf, masked, sums, pair_in, chip_in, half, half_in, prob, inv_own, prob_in, inv, acc, raw_in,
     far, far_in, joint, joint_in, tot, tot_z, tot2, tot_x, grand,
     sem_load, sem_sent, sem_got, sem_f, sem_j,
 ):
     s, t = lax.axis_index("shard"), lax.axis_index("task")
     expert = lax.div(s, GROUP)
     member = lax.rem(s, GROUP)
+    core = lax.rem(s, 2)
     first = expert * GROUP
     late = lax.rem(expert, 2)
     hub = (expert - late) * GROUP
@@ -45,6 +46,9 @@
 
     def at_x(d):
         return (lax.rem(s + 2 * GROUP * d, SHARDS), t)
+
+    def block_of(owner):
+        return pl.ds(pl.multiple_of(owner * 2 * HALF, 2 * HALF), 2 * HALF)
 
     def at_group(d):
         return (first + lax.rem(member + d, GROUP), t)
@@ -63,7 +67,7 @@
     def shares(ref):
         return {0: ref.at[pl.ds(0, 1)], 1: ref.at[:, pl.ds(0, 2)], 2: ref.at[pl.ds(0, 2)], 4: ref}[RAW]
 
-    SUM, TOTAL, TOTAL_X, GRAND, PROB, PROB_Y, ENTRY, FAR, JOINT = range(9)
+    PAIR, CHIP, WHOLE, TOTAL, TOTAL_X, GRAND, PROB_Y, ENTRY, FAR, JOINT = range(10)
 
     barrier = pltpu.get_barrier_semaphore()
 
@@ -81,46 +85,74 @@
         for m in range(GROUP):
             greet((other + m, t))
 
-    loads = [
-        pltpu.make_async_copy(limit_in, limit, sem_load.at[0]),
-        pltpu.make_async_copy(delta.at[0, 0], dbuf.at[0], sem_load.at[1]),
-        pltpu.make_async_copy(score.at[0, 0], sbuf.at[0], sem_load.at[2]),
-        pltpu.make_async_copy(delta.at[0, pl.ds(1, LAYERS - 1)], dbuf.at[pl.ds(1, LAYERS - 1)], sem_load.at[3]),
-        pltpu.make_async_copy(score.at[0, pl.ds(1, LAYERS - 1)], sbuf.at[pl.ds(1, LAYERS - 1)], sem_load.at[4]),
-    ]
+    up, down, far_owner = lax.rem(t + 1, TASKS), lax.rem(t + 3, TASKS), lax.rem(t + 2, TASKS)
+    pieces = [(limit_in, limit)]
+    for owner in (up, down):
+        pieces.append((delta.at[0, 0, :, block_of(owner)], dbuf.at[0, :, block_of(owner)]))
+        pieces.append((score.at[0, 0, :, block_of(owner)], sbuf.at[0, :, block_of(owner)]))
+    for owner in (far_owner, t):
+        pieces.append((delta.at[0, 0, :, block_of(owner)], dbuf.at[0, :, block_of(owner)]))
+    rest_l = pl.ds(1, LAYERS - 1)
+    pieces.append((delta.at[0, rest_l], dbuf.at[rest_l]))
+    for owner in (far_owner, t):
+        pieces.append((score.at[0, 0, :, block_of(owner)], sbuf.at[0, :, block_of(owner)]))
+    pieces.append((score.at[0, rest_l], sbuf.at[rest_l]))
+    loads = [pltpu.make_async_copy(src, dst, sem_load.at[i]) for i, (src, dst) in enumerate(pieces)]
     for load in loads:
         load.start()
+
+    row = lax.broadcasted_iota(jnp.int32, (8, LANES), 0)
+    bits = [lax.rem(lax.div(row, 2**k), 2) == 0 for k in range(3)]
 
     def sum_layer(l):
         def body(i, carry):
             b, h = lax.div(i, 2), lax.rem(i, 2)
-            for j in range(PARTS):
-                cols = pl.ds(pl.multiple_of(i * HALF + j * LANES, LANES), LANES)
-                change = jnp.abs(dbuf[l, :, cols].astype(F32))
-                sums[b, l, h, j : j + 1, :] = jnp.sum(change, axis=0, keepdims=True)
+            for j0 in range(0, PARTS, 8):
+                parts = []
+                for j in range(j0, j0 + 8):
+                    cols = pl.ds(pl.multiple_of(i * HALF + j * LANES, LANES), LANES)
+                    change = jnp.abs(dbuf[l, :, cols].astype(F32))
+                    parts.append(change[:8] + change[8:])
+                for k, even in enumerate(bits):
+                    parts = [
+                        jnp.where(even, a, b_) + pltpu.roll(jnp.where(even, b_, a), 2**k, 0)
+                        for a, b_ in zip(parts[::2], parts[1::2])
+                    ]
+                sums[h, b, l, j0 : j0 + 8, :] = parts[0]
             return carry
 
         lax.fori_loop(0, 2 * TASKS, body, 0)
 
+    def mask_half(l, i):
+        b, h = lax.div(i, 2), lax.rem(i, 2)
+        own_limit = limit[0, l, expert]
+        for j in range(PARTS):
+            cols = pl.ds(pl.multiple_of(i * HALF + j * LANES, LANES), LANES)
+            keep = sbuf[l, :, cols] < own_limit
+            masked[b, l, h, :, j * LANES : (j + 1) * LANES] = jnp.where(
+                keep, dbuf[l, :, cols].astype(F32), F32(0.0)
+            ).astype(BF16)
+
+    def mask_block(l, owner):
+        def body(i, carry):
+            mask_half(l, 2 * owner + i)
+            return carry
+
+        lax.fori_loop(0, 2, body, 0)
+
     def mask_layer(l):
-        own_limit = limit[0, l, expert]
-
         def body(i, carry):
-            b, h = lax.div(i, 2), lax.rem(i, 2)
-            for j in range(PARTS):
-                cols = pl.ds(pl.multiple_of(i * HALF + j * LANES, LANES), LANES)
-                keep = sbuf[l, :, cols] < own_limit
-                masked[b, l, h, :, j * LANES : (j + 1) * LANES] = jnp.where(
-                    keep, dbuf[l, :, cols].astype(F32), F32(0.0)
-                ).astype(BF16)
+            mask_half(l, i)
             return carry
 
         lax.fori_loop(0, 2 * TASKS, body, 0)
 
     flight = []
 
-    def send_raw(l):
-        for d in (1, 3, 2) if l < RAW else (1, 3):
+    def send_raw(l, ds=(1, 3, 2)):
+        for d in ds:
+            if d == 2 and l >= RAW:
+                continue
             owner = lax.rem(t + d, TASKS)
             if l < RAW:
                 flight.append(send(masked.at[owner, l], raw_in.at[d - 1, l], ENTRY, at_task(d)))
@@ -132,20 +164,27 @@
         for load in loads[:3]:
             load.wait()
     with jax.named_scope("mask0"):
-        mask_layer(0)
+        mask_block(0, up)
     with jax.named_scope("bar"):
         pl.semaphore_wait(barrier, 9 + late)
-    send_raw(0)
+    send_raw(0, (1,))
+    with jax.named_scope("mask1"):
+        for load in loads[3:5]:
+            load.wait()
+        mask_block(0, down)
+    send_raw(0, (3,))
     with jax.named_scope("sums"):
-        sum_layer(0)
-        loads[3].wait()
-        for l in range(1, LAYERS):
+        for load in loads[5:8]:
+            load.wait()
+        for l in range(LAYERS):
             sum_layer(l)
 
+    send(sums.at[1 - core], pair_in, PAIR, at_group(1 - 2 * core + GROUP))
+
     for l in range(LAYERS):
-        whole = sums[0, l, 0] + sums[0, l, 1]
+        whole = sums[0, 0, l] + sums[1, 0, l]
         for b in range(1, TASKS):
-            whole = whole + sums[b, l, 0] + sums[b, l, 1]
+            whole = whole + sums[0, b, l] + sums[1, b, l]
         tot[l : l + 1, :] = jnp.sum(whole, axis=0, keepdims=True)
     tot[LAYERS:, :] = jnp.zeros((8 - LAYERS, LANES), F32)
 
@@ -159,16 +198,22 @@
         for m in range(GROUP):
             send(tot, tot_z.at[GROUP - 1 + member], TOTAL, (other + m, t))
 
-    for d in range(1, GROUP):
-        send(sums.at[lax.rem(member + d, GROUP)], sums_in.at[d - 1], SUM, at_group(d))
-
     with jax.named_scope("masks"):
-        loads[4].wait()
+        for load, owner in ((loads[8], far_owner), (loads[9], t)):
+            load.wait()
+            mask_block(0, owner)
+        send_raw(0, (2,))
+        loads[10].wait()
         for l in range(1, LAYERS):
             mask_layer(l)
             send_raw(l)
 
-    with jax.named_scope("totals"):
+    with jax.named_scope("waitpair"):
+        wait(pair_in, sem_got.at[PAIR])
+    sums[core] = sums[core] + pair_in[...]
+    send(sums.at[core], chip_in, CHIP, at_group(2))
+
+    with jax.named_scope("totals1"):
 
         @pl.when(late == 0)
         def _():
@@ -179,6 +224,15 @@
             tot2[...] = whole
             for d in (1, 2, 3):
                 send(tot2, tot_x.at[d - 1], TOTAL_X, at_x(d))
+
+    with jax.named_scope("waitchip"):
+        wait(chip_in, sem_got.at[CHIP])
+    half[...] = sums[core] + chip_in[...]
+    send(half, half_in, WHOLE, at_group(1 - 2 * core + GROUP))
+    with jax.named_scope("totals2"):
+
+        @pl.when(late == 0)
+        def _():
             wait(tot_x, sem_got.at[TOTAL_X])
             grand[...] = tot2[...] + tot_x[0] + tot_x[1] + tot_x[2]
             send(grand, grand, GRAND, (other + member, t))
@@ -188,28 +242,26 @@
             wait(grand, sem_got.at[GRAND])
 
     grand_mean = jnp.sum(grand[...], axis=1, keepdims=True) / F32(EXPERTS * ROWS * FF)
-    with jax.named_scope("waitsum"):
-        wait(sums_in, sem_got.at[SUM])
-
-    for l in range(LAYERS):
+    with jax.named_scope("waitwhole"):
+        wait(half_in, sem_got.at[WHOLE])
+
+    def make_prob(b, l):
         mean_l = jnp.broadcast_to(grand_mean[l : l + 1, :], (PARTS, LANES))
+        mine, theirs = half[b, l], half_in[b, l]
         for h in range(2):
-            column = sums[member, l, h] + sums_in[0, l, h] + sums_in[1, l, h] + sums_in[2, l, h]
-            column = column / F32(ROWS)
-            prob[member, l, h] = (0.2 + 0.7 * column / (column + mean_l)).astype(BF16)
-    for d in range(1, GROUP):
-        send(prob.at[member], prob.at[member], PROB, at_group(d))
-    with jax.named_scope("waitp"):
-        wait(prob.at[pl.ds(0, GROUP - 1)], sem_got.at[PROB])
+            column = jnp.where(core == h, mine, theirs) / F32(ROWS)
+            rounded = (0.2 + 0.7 * column / (column + mean_l)).astype(BF16)
+            prob[b, l, h] = rounded
+            inv_own[b, l, h] = 1.0 / rounded.astype(F32)
 
     def rescaled(block, tile, j):
         return block[:, j * LANES : (j + 1) * LANES].astype(F32) * tile[j : j + 1, :]
 
-    far_owner = lax.rem(t + 2, TASKS)
     with jax.named_scope("far"):
         for l in range(RAW, LAYERS):
+            make_prob(far_owner, l)
             for h in range(2):
-                tile = 1.0 / prob[far_owner, l, h].astype(F32)
+                tile = inv_own[far_owner, l, h]
                 for j in range(PARTS):
                     far[h, l - RAW, :, j * LANES : (j + 1) * LANES] = rescaled(
                         masked.at[far_owner, l, h], tile, j
@@ -217,6 +269,12 @@
                 flight.append(
                     send(far.at[h, l - RAW], far_in.at[h, l - RAW], FAR, at_task(3 if h else 1), sem_f.at[h, l - RAW])
                 )
+    with jax.named_scope("prob"):
+        for l in range(RAW):
+            make_prob(far_owner, l)
+        for owner in (up, down, t):
+            for l in range(LAYERS):
+                make_prob(owner, l)
     for d in (1, 3):
         owner, h = lax.rem(t + d, TASKS), 1 if d == 1 else 0
         if RAW < LAYERS:
@@ -229,7 +287,7 @@
     with jax.named_scope("own"):
         for l in range(LAYERS):
             for h in range(2):
-                tile = 1.0 / prob[t, l, h].astype(F32)
+                tile = inv_own[t, l, h]
                 for j in range(PARTS):
                     acc[l, h, :, j * LANES : (j + 1) * LANES] = rescaled(masked.at[t, l, h], tile, j)
 
@@ -238,7 +296,7 @@
             with jax.named_scope(f"waitfar#l={l}#h={h}"):
                 wait(far_in.at[h, l - RAW], sem_f.at[h, l - RAW])
             owner = lax.rem(t + (3 if h else 1), TASKS)
-            tile = 1.0 / prob[owner, l, h].astype(F32)
+            tile = inv_own[owner, l, h]
             for j in range(PARTS):
                 cols = slice(j * LANES, (j + 1) * LANES)
                 joint[h, l - RAW, :, cols] = (
@@ -291,8 +349,9 @@
         def _():
             wait(tot_z.at[pl.ds(0, GROUP)], sem_sent.at[TOTAL])
 
-        wait(sums_in, sem_sent.at[SUM])
-        wait(prob.at[pl.ds(0, GROUP - 1)], sem_sent.at[PROB])
+        wait(pair_in, sem_sent.at[PAIR])
+        wait(chip_in, sem_sent.at[CHIP])
+        wait(half, sem_sent.at[WHOLE])
         wait(shares(prob_in), sem_sent.at[PROB_Y])
         wait(shares(raw_in), sem_sent.at[ENTRY])
         if RAW < LAYERS:
@@ -313,9 +372,10 @@
             pltpu.VMEM((LAYERS, HERE, FF), BF16),
             pltpu.VMEM((LAYERS, HERE, FF), jnp.int32),
             pltpu.VMEM((TASKS, LAYERS, 2, HERE, HALF), BF16),
+            pltpu.VMEM((2, TASKS, LAYERS, PARTS, LANES), F32),
+            *[pltpu.VMEM((TASKS, LAYERS, PARTS, LANES), F32)] * 4,
+            pltpu.VMEM((TASKS, LAYERS, 2, PARTS, LANES), BF16),
             pltpu.VMEM((TASKS, LAYERS, 2, PARTS, LANES), F32),
-            pltpu.VMEM((GROUP - 1, LAYERS, 2, PARTS, LANES), F32),
-            pltpu.VMEM((TASKS, LAYERS, 2, PARTS, LANES), BF16),
             pltpu.VMEM((3, LAYERS, 2, PARTS, LANES), BF16),
             pltpu.VMEM((3, LAYERS, 2, PARTS, LANES), F32),
             pltpu.VMEM((LAYERS, 2, HERE, HALF), F32),
@@ -326,9 +386,9 @@
             pltpu.VMEM((8, LANES), F32),
             pltpu.VMEM((3, 8, LANES), F32),
             pltpu.VMEM((8, LANES), F32),
-            dma((5,)),
-            dma((9,)),
-            dma((7,)),
+            dma((11,)),
+            dma((10,)),
+            dma((8,)),
             dma((2, REST)),
             dma((2, REST)),
         ],

time: 29.8 us -> 27.6 us (0.926)
  Pallas kernels: 28.9 us -> 26.7 us
    pallas_call x1, Pallas kernels: 28.9 us -> 26.7 us  [on_device(): pl.pallas_call(kernel, out_shape=jax.ShapeDtypeStruct((LAYERS, HERE, 2 *...]
where the time goes in v3:
time: 27.6 us; the launch traced here: 27.5 us
  Pallas kernels  26.7 us (97%)
  local copies, waits for them, and re-layouts  0.8 us (3%)
    pallas_call x1, Pallas kernels, on_device(): pl.pallas_call(kernel, out_shape=jax.ShapeDtypeStruct((LAYERS, HERE, 2 *...  26.7 us
    unnamed x1, local copies, waits for them, and re-layouts  0.8 us

profile of v3, /device:TPU:64, one launch (start us, length us, event | category | flops | bytes accessed | tf_op | source)
XLA Modules:
  0.0 27.5 jit_solution(8312307530713431009)
XLA Ops:
  0.0 26.7 %shard_map.37 = bf16[4,16,4096]{2,1,0:T(8,128)(2,1)S(1)} custom-call(bf16[1,4,16,16384]{3,2,1,0:T(8,128)(2,1)} %delta.1, s32[1,4,16,16384]{3,2,1,0:T(8,128)} %score.1, s32[1,4,8]{2,1,0:T(4,128)} %limit_in.1), custom_call_target="tpu_custom_call" | custom-call | tf_op jit(solution)/shard_map/pallas_call | solution.py:365
  26.7 0.8 %copy.5 = bf16[4,16,4096]{2,1,0:T(8,128)(2,1)} copy(bf16[4,16,4096]{2,1,0:T(8,128)(2,1)S(1)} %shard_map.37) | data formatting | bytes 1048576

commit v4 on v3

--- a/solution.py
+++ b/solution.py
@@ -28,9 +28,9 @@
 
 def kernel(
     delta, score, limit_in, out,
-    limit, dbuf, sbuf, masked, sums, pair_in, chip_in, half, half_in, prob, inv_own, prob_in, inv, acc, raw_in,
+    limit, dbuf, sbuf, masked, sums, pair_in, chip_out, chip_in, half, half_in, prob, inv_own, prob_in, inv, acc, raw_in,
     far, far_in, joint, joint_in, tot, tot_z, tot2, tot_x, grand,
-    sem_load, sem_sent, sem_got, sem_f, sem_j,
+    sem_load, sem_sent, sem_got, sem_f, sem_j, sem_near,
 ):
     s, t = lax.axis_index("shard"), lax.axis_index("task")
     expert = lax.div(s, GROUP)
@@ -38,8 +38,8 @@
     core = lax.rem(s, 2)
     first = expert * GROUP
     late = lax.rem(expert, 2)
-    hub = (expert - late) * GROUP
-    other = hub + (1 - late) * GROUP
+    other = (expert + 1 - 2 * late) * GROUP
+    hub = jnp.logical_and(late == 0, core == 1)
 
     def at_task(d):
         return (s, lax.rem(t + d, TASKS))
@@ -47,19 +47,22 @@
     def at_x(d):
         return (lax.rem(s + 2 * GROUP * d, SHARDS), t)
 
+    def at_other(m):
+        return (other + m, t)
+
     def block_of(owner):
         return pl.ds(pl.multiple_of(owner * 2 * HALF, 2 * HALF), 2 * HALF)
 
     def at_group(d):
         return (first + lax.rem(member + d, GROUP), t)
 
-    def send(src, dst, kind, to, got=None):
+    def send(src, dst, kind, to, got=None, done=False):
         copy = pltpu.make_async_remote_copy(
             src_ref=src, dst_ref=dst, send_sem=sem_sent.at[kind], recv_sem=sem_got.at[kind] if got is None else got,
             device_id=to, device_id_type=MESH,
         )
         copy.start()
-        return copy
+        return None if done else copy
 
     def wait(ref, sem):
         pltpu.make_async_copy(ref, ref, sem).wait()
@@ -74,16 +77,18 @@
     def greet(to):
         pl.semaphore_signal(barrier, inc=1, device_id=to, device_id_type=MESH)
 
+    wide = t < 2
+    at_x0 = lax.div(s, 2 * GROUP)
     for d in (1, 2, 3):
         greet(at_task(d))
-        greet(at_group(d))
-
-    @pl.when(late == 0)
+        pl.when(jnp.logical_or(wide, member + d < GROUP))(functools.partial(greet, at_group(d)))
+
+    @pl.when(hub)
     def _():
         for d in (1, 2, 3):
-            greet(at_x(d))
+            pl.when(jnp.logical_or(wide, at_x0 + d < SHARDS // (2 * GROUP)))(functools.partial(greet, at_x(d)))
         for m in range(GROUP):
-            greet((other + m, t))
+            greet(at_other(m))
 
     up, down, far_owner = lax.rem(t + 1, TASKS), lax.rem(t + 3, TASKS), lax.rem(t + 2, TASKS)
     pieces = [(limit_in, limit)]
@@ -92,11 +97,12 @@
         pieces.append((score.at[0, 0, :, block_of(owner)], sbuf.at[0, :, block_of(owner)]))
     for owner in (far_owner, t):
         pieces.append((delta.at[0, 0, :, block_of(owner)], dbuf.at[0, :, block_of(owner)]))
-    rest_l = pl.ds(1, LAYERS - 1)
-    pieces.append((delta.at[0, rest_l], dbuf.at[rest_l]))
+    for l in range(1, LAYERS):
+        pieces.append((delta.at[0, l], dbuf.at[l]))
     for owner in (far_owner, t):
         pieces.append((score.at[0, 0, :, block_of(owner)], sbuf.at[0, :, block_of(owner)]))
-    pieces.append((score.at[0, rest_l], sbuf.at[rest_l]))
+    for l in range(1, LAYERS):
+        pieces.append((score.at[0, l], sbuf.at[l]))
     loads = [pltpu.make_async_copy(src, dst, sem_load.at[i]) for i, (src, dst) in enumerate(pieces)]
     for load in loads:
         load.start()
@@ -165,21 +171,47 @@
             load.wait()
     with jax.named_scope("mask0"):
         mask_block(0, up)
-    with jax.named_scope("bar"):
-        pl.semaphore_wait(barrier, 9 + late)
-    send_raw(0, (1,))
-    with jax.named_scope("mask1"):
+
+    def all_sums():
+        for l in range(LAYERS):
+            for load in loads[5:7] if l == 0 else loads[6 + l : 7 + l]:
+                load.wait()
+            sum_layer(l)
+
+    def mask_down():
         for load in loads[3:5]:
             load.wait()
         mask_block(0, down)
+
+    with jax.named_scope("sums0"):
+
+        @pl.when(t < 2)
+        def _():
+            mask_down()
+            all_sums()
+
+    with jax.named_scope("bar"):
+        met = jnp.where(wide, GROUP - 1, member) + 2 * late + jnp.where(hub, jnp.where(wide, GROUP - 1, at_x0), 0)
+        pl.semaphore_wait(barrier, TASKS - 1 + met)
+    send_raw(0, (1,))
+
+    @pl.when(jnp.logical_not(wide))
+    def _():
+        for d in (1, 2, 3):
+            for back, peer in (
+                (member - d >= 0, at_group(4 - d)),
+                (jnp.logical_and(hub, at_x0 - d >= 0), at_x(4 - d)),
+            ):
+
+                @pl.when(back)
+                def _():
+                    pl.semaphore_signal(sem_near, inc=1, device_id=peer, device_id_type=MESH)
+
+    with jax.named_scope("mask1"):
+        pl.when(t >= 2)(mask_down)
     send_raw(0, (3,))
-    with jax.named_scope("sums"):
-        for load in loads[5:8]:
-            load.wait()
-        for l in range(LAYERS):
-            sum_layer(l)
-
-    send(sums.at[1 - core], pair_in, PAIR, at_group(1 - 2 * core + GROUP))
+    with jax.named_scope("sums1"):
+        pl.when(t >= 2)(all_sums)
 
     for l in range(LAYERS):
         whole = sums[0, 0, l] + sums[1, 0, l]
@@ -188,34 +220,47 @@
         tot[l : l + 1, :] = jnp.sum(whole, axis=0, keepdims=True)
     tot[LAYERS:, :] = jnp.zeros((8 - LAYERS, LANES), F32)
 
+    @pl.when(late == 1)
+    def _():
+        for m in (1, 3):
+            send(tot, tot_z.at[GROUP - 1 + member], TOTAL, at_other(m))
+
+    with jax.named_scope("near"):
+
+        to_come = GROUP - 1 - member + jnp.where(hub, GROUP - 1 - at_x0, 0)
+
+        @pl.when(jnp.logical_and(jnp.logical_not(wide), to_come > 0))
+        def _():
+            pl.semaphore_wait(sem_near, to_come)
+
+    send(sums.at[1 - core], pair_in, PAIR, at_group(1 - 2 * core + GROUP))
+
     @pl.when(late == 0)
     def _():
         for d in range(1, GROUP):
-            send(tot, tot_z.at[d - 1], TOTAL, at_group(d))
-
-    @pl.when(late == 1)
-    def _():
-        for m in range(GROUP):
-            send(tot, tot_z.at[GROUP - 1 + member], TOTAL, (other + m, t))
+            pl.when(lax.rem(member + d, 2) == 1)(
+                functools.partial(send, tot, tot_z.at[d - 1], TOTAL, at_group(d), done=True)
+            )
 
     with jax.named_scope("masks"):
-        for load, owner in ((loads[8], far_owner), (loads[9], t)):
+        for load, owner in ((loads[10], far_owner), (loads[11], t)):
             load.wait()
             mask_block(0, owner)
         send_raw(0, (2,))
-        loads[10].wait()
         for l in range(1, LAYERS):
+            loads[11 + l].wait()
             mask_layer(l)
             send_raw(l)
 
     with jax.named_scope("waitpair"):
         wait(pair_in, sem_got.at[PAIR])
-    sums[core] = sums[core] + pair_in[...]
-    send(sums.at[core], chip_in, CHIP, at_group(2))
+    half[...] = sums[core] + pair_in[...]
+    chip_out[...] = half[...]
+    send(chip_out, chip_in, CHIP, at_group(2))
 
     with jax.named_scope("totals1"):
 
-        @pl.when(late == 0)
+        @pl.when(hub)
         def _():
             wait(tot_z, sem_got.at[TOTAL])
             whole = tot[...]
@@ -227,17 +272,19 @@
 
     with jax.named_scope("waitchip"):
         wait(chip_in, sem_got.at[CHIP])
-    half[...] = sums[core] + chip_in[...]
+    half[...] = chip_out[...] + chip_in[...]
     send(half, half_in, WHOLE, at_group(1 - 2 * core + GROUP))
     with jax.named_scope("totals2"):
 
-        @pl.when(late == 0)
+        @pl.when(hub)
         def _():
             wait(tot_x, sem_got.at[TOTAL_X])
             grand[...] = tot2[...] + tot_x[0] + tot_x[1] + tot_x[2]
-            send(grand, grand, GRAND, (other + member, t))
-
-        @pl.when(late == 1)
+            send(grand, grand, GRAND, at_other(GROUP - 1 - member))
+            send(grand, grand, GRAND, at_other(GROUP - member))
+            send(grand, grand, GRAND, at_group(GROUP - 1))
+
+        @pl.when(jnp.logical_not(hub))
         def _():
             wait(grand, sem_got.at[GRAND])
 
@@ -338,16 +385,15 @@
                 ).astype(BF16)
 
     with jax.named_scope("waitsend"):
-
-        @pl.when(late == 0)
-        def _():
-            wait(tot_z.at[pl.ds(0, GROUP - 1)], sem_sent.at[TOTAL])
+        @pl.when(hub)
+        def _():
+            wait(tot_z.at[0], sem_sent.at[TOTAL])
             wait(tot_x, sem_sent.at[TOTAL_X])
-            wait(grand, sem_sent.at[GRAND])
-
-        @pl.when(late == 1)
-        def _():
-            wait(tot_z.at[pl.ds(0, GROUP)], sem_sent.at[TOTAL])
+            wait(tot_x, sem_sent.at[GRAND])
+
+        @pl.when(jnp.logical_not(hub))
+        def _():
+            wait(tot_z.at[pl.ds(0, 2)], sem_sent.at[TOTAL])
 
         wait(pair_in, sem_sent.at[PAIR])
         wait(chip_in, sem_sent.at[CHIP])
@@ -373,6 +419,7 @@
             pltpu.VMEM((LAYERS, HERE, FF), jnp.int32),
             pltpu.VMEM((TASKS, LAYERS, 2, HERE, HALF), BF16),
             pltpu.VMEM((2, TASKS, LAYERS, PARTS, LANES), F32),
+            pltpu.VMEM((TASKS, LAYERS, PARTS, LANES), F32),
             *[pltpu.VMEM((TASKS, LAYERS, PARTS, LANES), F32)] * 4,
             pltpu.VMEM((TASKS, LAYERS, 2, PARTS, LANES), BF16),
             pltpu.VMEM((TASKS, LAYERS, 2, PARTS, LANES), F32),
@@ -386,11 +433,12 @@
             pltpu.VMEM((8, LANES), F32),
             pltpu.VMEM((3, 8, LANES), F32),
             pltpu.VMEM((8, LANES), F32),
-            dma((11,)),
+            dma((15,)),
             dma((10,)),
             dma((8,)),
             dma((2, REST)),
             dma((2, REST)),
+            pltpu.SemaphoreType.REGULAR,
         ],
         compiler_params=pltpu.CompilerParams(
             collective_id=0, has_side_effects=True, vmem_limit_bytes=32 * 1024 * 1024

time: 27.6 us -> 26.6 us (0.964)
  the two profiles are of different devices: /device:TPU:64 before, /device:TPU:0 now
where the time goes in v4:
time: 26.6 us; the launch traced here: 26.4 us
  Pallas kernels  25.5 us (96%)
  local copies, waits for them, and re-layouts  0.8 us (3%)
    pallas_call x1, Pallas kernels, on_device(): pl.pallas_call(kernel, out_shape=jax.ShapeDtypeStruct((LAYERS, HERE, 2 *...  25.5 us
    unnamed x1, local copies, waits for them, and re-layouts  0.8 us

profile of v4, /device:TPU:0, one launch (start us, length us, event | category | flops | bytes accessed | tf_op | source)
XLA Modules:
  0.0 26.4 jit_solution(43261936973627923)
XLA Ops:
  0.0 25.5 %shard_map.37 = bf16[4,16,4096]{2,1,0:T(8,128)(2,1)S(1)} custom-call(bf16[1,4,16,16384]{3,2,1,0:T(8,128)(2,1)} %delta.1, s32[1,4,16,16384]{3,2,1,0:T(8,128)} %score.1, s32[1,4,8]{2,1,0:T(4,128)} %limit_in.1), custom_call_target="tpu_custom_call" | custom-call | tf_op jit(solution)/shard_map/pallas_call | solution.py:411
  25.6 0.8 %copy.5 = bf16[4,16,4096]{2,1,0:T(8,128)(2,1)} copy(bf16[4,16,4096]{2,1,0:T(8,128)(2,1)S(1)} %shard_map.37) | data formatting | bytes 1048576

commit v5 on v4

v5 whole, which is shorter than its diff:
```python
import functools

import jax
import jax.numpy as jnp
from jax import lax
from jax.experimental import pallas as pl
from jax.experimental.pallas import tpu as pltpu
from jax.sharding import PartitionSpec as P

EXPERTS = 8
ROWS = 64
FF = 16384
LAYERS = 4
TASKS = 4
SHARDS = 32
GROUP = 4
HERE = 16
HALF = 2048
LANES = 128
PARTS = HALF // LANES
HELD = 1

MESH = pl.DeviceIdType.MESH
F32 = jnp.float32
BF16 = jnp.bfloat16


def kernel(
    delta, score, limit_in, out,
    limit, dbuf, sbuf, masked, sums, pair_in, chip_out, chip_in, half, half_in, prob, inv_own, prob_in, far_prob, acc, raw_in,
    far_in, joint, joint_in, tot, tot_z, tot2, tot_x, grand,
    sem_load, sem_sent, sem_got, sem_j, sem_near, sem_line,
):
    s, t = lax.axis_index("shard"), lax.axis_index("task")
    expert = lax.div(s, GROUP)
    member = lax.rem(s, GROUP)
    core = lax.rem(s, 2)
    first = expert * GROUP
    late = lax.rem(expert, 2)
    other = (expert + 1 - 2 * late) * GROUP
    hub = jnp.logical_and(late == 0, core == 1)

    def at_task(d):
        return (s, lax.rem(t + d, TASKS))

    def at_x(d):
        return (lax.rem(s + 2 * GROUP * d, SHARDS), t)

    def at_other(m):
        return (other + m, t)

    def block_of(owner):
        return pl.ds(pl.multiple_of(owner * 2 * HALF, 2 * HALF), 2 * HALF)

    def at_group(d):
        return (first + lax.rem(member + d, GROUP), t)

    def send(src, dst, kind, sent, to, got=None):
        copy = pltpu.make_async_remote_copy(
            src_ref=src, dst_ref=dst, send_sem=sem_sent.at[sent], recv_sem=sem_got.at[kind] if got is None else got,
            device_id=to, device_id_type=MESH,
        )
        copy.start()

    def wait(ref, sem):
        pltpu.make_async_copy(ref, ref, sem).wait()

    PAIR, CHIP, WHOLE, TOTAL, TOTAL_X, GRAND, PROB_F, PROB_Y, NEAR, FAR = range(10)
    COLUMNS, TOTALS, PROBS, ENTRIES = range(4)

    barrier = pltpu.get_barrier_semaphore()

    def greet(to):
        pl.semaphore_signal(barrier, inc=1, device_id=to, device_id_type=MESH)

    wide = t < 2
    at_x0 = lax.div(s, 2 * GROUP)
    greet(at_task(1))
    greet(at_task(3))
    for d in (1, 2, 3):
        pl.when(jnp.logical_or(wide, member + d < GROUP))(functools.partial(greet, at_group(d)))

    @pl.when(hub)
    def _():
        for d in (1, 2, 3):
            pl.when(jnp.logical_or(wide, at_x0 + d < SHARDS // (2 * GROUP)))(functools.partial(greet, at_x(d)))
        for m in range(GROUP):
            greet(at_other(m))

    up, down, far_owner = lax.rem(t + 1, TASKS), lax.rem(t + 3, TASKS), lax.rem(t + 2, TASKS)
    first_d, first_s = delta.at[0, 0], score.at[0, 0]
    pieces = [(limit_in, limit, 0)]
    pieces.append((first_d.at[:, block_of(far_owner)], dbuf.at[0, :, block_of(far_owner)], 1))
    pieces.append((first_s.at[:, block_of(far_owner)], sbuf.at[0, :, block_of(far_owner)], 1))
    for owner in (up, down):
        pieces.append((first_d.at[:, block_of(owner)], dbuf.at[0, :, block_of(owner)], 2))
    pieces.append((first_d.at[:, block_of(t)], dbuf.at[0, :, block_of(t)], 3))
    for l in range(1, LAYERS):
        pieces.append((delta.at[0, l], dbuf.at[l], 3 + l))
    for owner in (up, down):
        pieces.append((first_s.at[:, block_of(owner)], sbuf.at[0, :, block_of(owner)], 7))
    pieces.append((first_s.at[:, block_of(t)], sbuf.at[0, :, block_of(t)], 8))
    pieces.append((score.at[0, pl.ds(1, LAYERS - 1)], sbuf.at[pl.ds(1, LAYERS - 1)], 9))
    loads = [pltpu.make_async_copy(src, dst, sem_load.at[i]) for src, dst, i in pieces]
    for load in loads:
        load.start()

    place = lax.broadcasted_iota(jnp.int32, (PARTS, PARTS * HERE), 1) - HERE * lax.broadcasted_iota(
        jnp.int32, (PARTS, PARTS * HERE), 0
    )
    pick = jnp.where(jnp.logical_and(place >= 0, place < HERE), F32(1.0), F32(0.0)).astype(BF16)

    def sum_layer(l):
        def body(i, carry):
            b, h = lax.div(i, 2), lax.rem(i, 2)
            blocks = [
                jnp.abs(dbuf[l, :, pl.ds(pl.multiple_of(i * HALF + j * LANES, LANES), LANES)]) for j in range(PARTS)
            ]
            sums[h, b, l] = jnp.dot(pick, jnp.concatenate(blocks, axis=0), preferred_element_type=F32)
            return carry

        lax.fori_loop(0, 2 * TASKS, body, 0, unroll=True)

    def mask_half(l, i):
        b, h = lax.div(i, 2), lax.rem(i, 2)
        own_limit = limit[0, l, expert]
        for j in range(PARTS):
            cols = pl.ds(pl.multiple_of(i * HALF + j * LANES, LANES), LANES)
            keep = sbuf[l, :, cols] < own_limit
            masked[b, l, h, :, j * LANES : (j + 1) * LANES] = jnp.where(
                keep, dbuf[l, :, cols].astype(F32), F32(0.0)
            ).astype(BF16)

    def mask_block(l, owner):
        def body(i, carry):
            mask_half(l, 2 * owner + i)
            return carry

        lax.fori_loop(0, 2, body, 0)

    def mask_layer(l):
        def body(i, carry):
            mask_half(l, i)
            return carry

        lax.fori_loop(0, 2 * TASKS, body, 0)

    def send_far(l):
        for h in range(2):
            send(masked.at[far_owner, l, h], far_in.at[h, l], FAR, ENTRIES, at_task(3 if h else 1))

    def send_near(l):
        for d, owner, h in ((1, up, 1), (3, down, 0)):
            send(masked.at[owner, l, h], raw_in.at[h, l], NEAR, ENTRIES, at_task(d))

    with jax.named_scope("load"):
        loads[0].wait()
        wait(sbuf.at[0, :, pl.ds(0, 3 * HALF)], sem_load.at[1])
    with jax.named_scope("mask0"):
        mask_block(0, far_owner)

    def all_sums():
        wait(dbuf.at[0, :, pl.ds(0, 4 * HALF)], sem_load.at[2])
        for l in range(LAYERS):
            wait(dbuf.at[l] if l else dbuf.at[0, :, pl.ds(0, 2 * HALF)], sem_load.at[3 + l])
            sum_layer(l)

    def mask_near():
        wait(sbuf.at[0, :, pl.ds(0, 4 * HALF)], sem_load.at[7])
        mask_block(0, up)
        mask_block(0, down)

    with jax.named_scope("sums0"):

        @pl.when(t < 2)
        def _():
            all_sums()
            mask_near()

    with jax.named_scope("bar"):
        met = jnp.where(wide, GROUP - 1, member) + 2 * late + jnp.where(hub, jnp.where(wide, GROUP - 1, at_x0), 0)
        pl.semaphore_wait(barrier, 2 + met)
    send_far(0)

    @pl.when(jnp.logical_not(wide))
    def _():
        for d in (1, 2, 3):
            for back, peer, sem in (
                (member - d >= 0, at_group(4 - d), sem_near),
                (jnp.logical_and(hub, at_x0 - d >= 0), at_x(4 - d), sem_line),
            ):

                @pl.when(back)
                def _():
                    pl.semaphore_signal(sem, inc=1, device_id=peer, device_id_type=MESH)

    with jax.named_scope("sums1"):

        @pl.when(t >= 2)
        def _():
            all_sums()
            mask_near()

    send_near(0)

    for l in range(LAYERS):
        whole = sums[0, 0, l] + sums[1, 0, l]
        for b in range(1, TASKS):
            whole = whole + sums[0, b, l] + sums[1, b, l]
        tot[l : l + 1, :] = jnp.sum(whole, axis=0, keepdims=True)
    tot[LAYERS:, :] = jnp.zeros((8 - LAYERS, LANES), F32)

    @pl.when(late == 1)
    def _():
        for m in (1, 3):
            send(tot, tot_z.at[GROUP - 1 + member], TOTAL, TOTALS, at_other(m))

    with jax.named_scope("near"):

        to_come = GROUP - 1 - member

        @pl.when(jnp.logical_and(jnp.logical_not(wide), to_come > 0))
        def _():
            pl.semaphore_wait(sem_near, to_come)

    send(sums.at[1 - core], pair_in, PAIR, COLUMNS, at_group(1 - 2 * core + GROUP))

    @pl.when(late == 0)
    def _():
        for d in range(1, GROUP):
            pl.when(lax.rem(member + d, 2) == 1)(
                functools.partial(send, tot, tot_z.at[d - 1], TOTAL, TOTALS, at_group(d))
            )

    with jax.named_scope("masks"):
        wait(sbuf.at[0, :, pl.ds(0, 2 * HALF)], sem_load.at[8])
        mask_block(0, t)
        wait(sbuf.at[pl.ds(1, LAYERS - 1)], sem_load.at[9])
        for l in range(1, LAYERS):
            mask_layer(l)
            send_far(l)
        for l in range(1, LAYERS - HELD):
            send_near(l)

    with jax.named_scope("waitpair"):
        wait(pair_in, sem_got.at[PAIR])
    half[...] = sums[core] + pair_in[...]
    chip_out[...] = half[...]
    send(chip_out, chip_in, CHIP, COLUMNS, at_group(2))

    with jax.named_scope("totals1"):

        @pl.when(hub)
        def _():
            wait(tot_z, sem_got.at[TOTAL])
            whole = tot[...]
            for d in range(2 * GROUP - 1):
                whole = whole + tot_z[d]
            tot2[...] = whole
            to_come_x = GROUP - 1 - at_x0

            @pl.when(jnp.logical_and(jnp.logical_not(wide), to_come_x > 0))
            def _():
                pl.semaphore_wait(sem_line, to_come_x)

            for d in (1, 2, 3):
                send(tot2, tot_x.at[d - 1], TOTAL_X, TOTALS, at_x(d))

    with jax.named_scope("waitchip"):
        wait(chip_in, sem_got.at[CHIP])
    half[...] = chip_out[...] + chip_in[...]
    send(half, half_in, WHOLE, COLUMNS, at_group(1 - 2 * core + GROUP))
    with jax.named_scope("totals2"):

        @pl.when(hub)
        def _():
            wait(tot_x, sem_got.at[TOTAL_X])
            grand[...] = tot2[...] + tot_x[0] + tot_x[1] + tot_x[2]
            send(grand, grand, GRAND, TOTALS, at_other(GROUP - 1 - member))
            send(grand, grand, GRAND, TOTALS, at_other(GROUP - member))
            send(grand, grand, GRAND, TOTALS, at_group(GROUP - 1))

        @pl.when(jnp.logical_not(hub))
        def _():
            wait(grand, sem_got.at[GRAND])

    grand_mean = jnp.sum(grand[...], axis=1, keepdims=True) / F32(EXPERTS * ROWS * FF)
    with jax.named_scope("waitwhole"):
        wait(half_in, sem_got.at[WHOLE])

    def make_prob(b, l):
        mean_l = jnp.broadcast_to(grand_mean[l : l + 1, :], (PARTS, LANES))
        mine, theirs = half[b, l], half_in[b, l]
        for h in range(2):
            column = jnp.where(core == h, mine, theirs) / F32(ROWS)
            rounded = (0.2 + 0.7 * column / (column + mean_l)).astype(BF16)
            prob[b, l, h] = rounded
            inv_own[b, l, h] = 1.0 / rounded.astype(F32)

    def rescaled(block, tile, j):
        return block[:, j * LANES : (j + 1) * LANES].astype(F32) * tile[j : j + 1, :]

    with jax.named_scope("farprob"):
        for l in range(LAYERS):
            make_prob(far_owner, l)
        for h in range(2):
            send(prob.at[far_owner, :, h], far_prob.at[h], PROB_F, PROBS, at_task(3 if h else 1))
    with jax.named_scope("prob"):
        for owner in (up, down, t):
            for l in range(LAYERS):
                make_prob(owner, l)
    for l in range(LAYERS - HELD, LAYERS):
        send_near(l)
    for d, owner, h in ((1, up, 1), (3, down, 0)):
        send(prob.at[owner, :, h], prob_in.at[h], PROB_Y, PROBS, at_task(d))

    with jax.named_scope("own"):
        for l in range(LAYERS):
            for h in range(2):
                tile = inv_own[t, l, h]
                for j in range(PARTS):
                    acc[l, h, :, j * LANES : (j + 1) * LANES] = rescaled(masked.at[t, l, h], tile, j)

    with jax.named_scope("waitfar"):
        wait(far_in, sem_got.at[FAR])
    with jax.named_scope("waitfarprob"):
        wait(far_prob, sem_got.at[PROB_F])
    for l in range(LAYERS):
        for h in range(2):
            owner = (up, down)[h]
            tile, far_tile = inv_own[owner, l, h], 1.0 / far_prob[h, l].astype(F32)
            for j in range(PARTS):
                joint[h, l, :, j * LANES : (j + 1) * LANES] = (
                    rescaled(masked.at[owner, l, h], tile, j) + rescaled(far_in.at[h, l], far_tile, j)
                ).astype(BF16)
            send(joint.at[h, l], joint_in.at[h, l], None, ENTRIES, at_task(3 if h else 1), sem_j.at[l])

    with jax.named_scope("waitpy"):
        wait(prob_in, sem_got.at[PROB_Y])
    with jax.named_scope("waitraw"):
        wait(raw_in, sem_got.at[NEAR])
    with jax.named_scope("raw"):
        for l in range(LAYERS):
            for h in range(2):
                tile = 1.0 / prob_in[h, l].astype(F32)
                for j in range(PARTS):
                    cols = slice(j * LANES, (j + 1) * LANES)
                    acc[l, h, :, cols] = acc[l, h, :, cols] + rescaled(raw_in.at[h, l], tile, j)
    for l in range(LAYERS):
        with jax.named_scope(f"waitjoint#l={l}"):
            wait(joint_in.at[:, l], sem_j.at[l])
        for h in range(2):
            for j in range(PARTS):
                cols = slice(j * LANES, (j + 1) * LANES)
                out[l, :, h * HALF + j * LANES : h * HALF + (j + 1) * LANES] = (
                    acc[l, h, :, cols] + joint_in[h, l, :, cols].astype(F32)
                ).astype(BF16)

    with jax.named_scope("waitsend"):
        @pl.when(hub)
        def _():
            wait(tot_z, sem_sent.at[TOTALS])

        @pl.when(jnp.logical_not(hub))
        def _():
            wait(tot_z.at[pl.ds(0, 2)], sem_sent.at[TOTALS])

        wait(masked.at[pl.ds(0, 3), 0], sem_sent.at[COLUMNS])
        wait(masked.at[0, 0, 0], sem_sent.at[PROBS])
        wait(masked.at[pl.ds(0, 3)], sem_sent.at[ENTRIES])


def on_device(task_deltas, rank_scores, keep_limits):
    dma = pltpu.SemaphoreType.DMA
    inputs = (pltpu.with_memory_space_constraint(x, pltpu.HBM) for x in (task_deltas, rank_scores, keep_limits))
    return pl.pallas_call(
        kernel,
        out_shape=jax.ShapeDtypeStruct((LAYERS, HERE, 2 * HALF), BF16),
        in_specs=[pl.BlockSpec(memory_space=pl.ANY)] * 3,
        out_specs=pl.BlockSpec(memory_space=pltpu.VMEM),
        scratch_shapes=[
            pltpu.SMEM((1, LAYERS, EXPERTS), jnp.int32),
            pltpu.VMEM((LAYERS, HERE, FF), BF16),
            pltpu.VMEM((LAYERS, HERE, FF), jnp.int32),
            pltpu.VMEM((TASKS, LAYERS, 2, HERE, HALF), BF16),
            pltpu.VMEM((2, TASKS, LAYERS, PARTS, LANES), F32),
            pltpu.VMEM((TASKS, LAYERS, PARTS, LANES), F32),
            *[pltpu.VMEM((TASKS, LAYERS, PARTS, LANES), F32)] * 4,
            pltpu.VMEM((TASKS, LAYERS, 2, PARTS, LANES), BF16),
            pltpu.VMEM((TASKS, LAYERS, 2, PARTS, LANES), F32),
            *[pltpu.VMEM((2, LAYERS, PARTS, LANES), BF16)] * 2,
            pltpu.VMEM((LAYERS, 2, HERE, HALF), F32),
            *[pltpu.VMEM((2, LAYERS, HERE, HALF), BF16)] * 4,
            pltpu.VMEM((8, LANES), F32),
            pltpu.VMEM((2 * GROUP - 1, 8, LANES), F32),
            pltpu.VMEM((8, LANES), F32),
            pltpu.VMEM((3, 8, LANES), F32),
            pltpu.VMEM((8, LANES), F32),
            dma((10,)),
            dma((4,)),
            dma((10,)),
            dma((LAYERS,)),
            pltpu.SemaphoreType.REGULAR,
            pltpu.SemaphoreType.REGULAR,
        ],
        compiler_params=pltpu.CompilerParams(
            collective_id=0, has_side_effects=True, vmem_limit_bytes=32 * 1024 * 1024
        ),
    )(*inputs)


def solution(mesh):
    in_specs = (P("task", None, "shard", None), P("task", None, "shard", None), P("task", None, None))
    return jax.shard_map(on_device, mesh=mesh, in_specs=in_specs, out_specs=P(None, "shard", "task"), check_vma=False)
```

time: 26.6 us -> 25.1 us (0.944)
  Pallas kernels: 25.5 us -> 24.2 us
    pallas_call x1, Pallas kernels: 25.5 us -> 24.2 us  [on_device(): pl.pallas_call(kernel, out_shape=jax.ShapeDtypeStruct((LAYERS, HERE, 2 *...]
where the time goes in v5:
time: 25.1 us; the launch traced here: 25 us
  Pallas kernels  24.2 us (96%)
  local copies, waits for them, and re-layouts  0.8 us (3%)
    pallas_call x1, Pallas kernels, on_device(): pl.pallas_call(kernel, out_shape=jax.ShapeDtypeStruct((LAYERS, HERE, 2 *...  24.2 us
    unnamed x1, local copies, waits for them, and re-layouts  0.8 us

profile of v5, /device:TPU:0, one launch (start us, length us, event | category | flops | bytes accessed | tf_op | source)
XLA Modules:
  0.0 25.0 jit_solution(465099585135949203)
XLA Ops:
  0.0 24.2 %shard_map.37 = bf16[4,16,4096]{2,1,0:T(8,128)(2,1)S(1)} custom-call(bf16[1,4,16,16384]{3,2,1,0:T(8,128)(2,1)} %delta.1, s32[1,4,16,16384]{3,2,1,0:T(8,128)} %score.1, s32[1,4,8]{2,1,0:T(4,128)} %limit_in.1), custom_call_target="tpu_custom_call" | custom-call | tf_op jit(solution)/shard_map/pallas_call | solution.py:376
  24.2 0.8 %copy.5 = bf16[4,16,4096]{2,1,0:T(8,128)(2,1)} copy(bf16[4,16,4096]{2,1,0:T(8,128)(2,1)S(1)} %shard_map.37) | data formatting | bytes 1048576

commit v6 on v5

--- a/solution.py
+++ b/solution.py
@@ -28,7 +28,7 @@
 def kernel(
     delta, score, limit_in, out,
     limit, dbuf, sbuf, masked, sums, pair_in, chip_out, chip_in, half, half_in, prob, inv_own, prob_in, far_prob, acc, raw_in,
-    far_in, joint, joint_in, tot, tot_z, tot2, tot_x, grand,
+    far_in, joint, joint_in, tot, tot_z, tot_l, tot2, tot_x, tot_f, grand,
     sem_load, sem_sent, sem_got, sem_j, sem_near, sem_line,
 ):
     s, t = lax.axis_index("shard"), lax.axis_index("task")
@@ -65,7 +65,7 @@
     def wait(ref, sem):
         pltpu.make_async_copy(ref, ref, sem).wait()
 
-    PAIR, CHIP, WHOLE, TOTAL, TOTAL_X, GRAND, PROB_F, PROB_Y, NEAR, FAR = range(10)
+    PAIR, CHIP, WHOLE, TOTAL, TOTAL_L, TOTAL_X, TOTAL_F, GRAND, PROB_F, PROB_Y, NEAR, FAR = range(12)
     COLUMNS, TOTALS, PROBS, ENTRIES = range(4)
 
     barrier = pltpu.get_barrier_semaphore()
@@ -77,16 +77,6 @@
     at_x0 = lax.div(s, 2 * GROUP)
     greet(at_task(1))
     greet(at_task(3))
-    for d in (1, 2, 3):
-        pl.when(jnp.logical_or(wide, member + d < GROUP))(functools.partial(greet, at_group(d)))
-
-    @pl.when(hub)
-    def _():
-        for d in (1, 2, 3):
-            pl.when(jnp.logical_or(wide, at_x0 + d < SHARDS // (2 * GROUP)))(functools.partial(greet, at_x(d)))
-        for m in range(GROUP):
-            greet(at_other(m))
-
     up, down, far_owner = lax.rem(t + 1, TASKS), lax.rem(t + 3, TASKS), lax.rem(t + 2, TASKS)
     first_d, first_s = delta.at[0, 0], score.at[0, 0]
     pieces = [(limit_in, limit, 0)]
@@ -105,6 +95,22 @@
     for load in loads:
         load.start()
 
+    for d in (1, 2, 3):
+        pl.when(jnp.logical_or(wide, member + d < GROUP))(functools.partial(greet, at_group(d)))
+
+    @pl.when(hub)
+    def _():
+        for d in (1, 2, 3):
+            pl.when(jnp.logical_or(wide, at_x0 + d < SHARDS // (2 * GROUP)))(functools.partial(greet, at_x(d)))
+        for m in range(GROUP):
+            greet(at_other(m))
+
+        @pl.when(at_x0 == 0)
+        def _():
+            for x in range(1, SHARDS // (2 * GROUP)):
+                for m in range(GROUP):
+                    greet(((2 * x + 1) * GROUP + m, t))
+
     place = lax.broadcasted_iota(jnp.int32, (PARTS, PARTS * HERE), 1) - HERE * lax.broadcasted_iota(
         jnp.int32, (PARTS, PARTS * HERE), 0
     )
@@ -178,7 +184,7 @@
             mask_near()
 
     with jax.named_scope("bar"):
-        met = jnp.where(wide, GROUP - 1, member) + 2 * late + jnp.where(hub, jnp.where(wide, GROUP - 1, at_x0), 0)
+        met = jnp.where(wide, GROUP - 1, member) + 2 * late * jnp.where(at_x0 > 0, 2, 1) + jnp.where(hub, jnp.where(wide, GROUP - 1, at_x0), 0)
         pl.semaphore_wait(barrier, 2 + met)
     send_far(0)
 
@@ -213,7 +219,12 @@
     @pl.when(late == 1)
     def _():
         for m in (1, 3):
-            send(tot, tot_z.at[GROUP - 1 + member], TOTAL, TOTALS, at_other(m))
+            send(tot, tot_l.at[member], TOTAL_L, TOTALS, at_other(m))
+
+        @pl.when(at_x0 > 0)
+        def _():
+            for m in (1, 3):
+                send(tot, tot_f.at[GROUP * (at_x0 - 1) + member], TOTAL_F, TOTALS, (m, t))
 
     with jax.named_scope("near"):
 
@@ -252,19 +263,27 @@
 
         @pl.when(hub)
         def _():
-            wait(tot_z, sem_got.at[TOTAL])
-            whole = tot[...]
-            for d in range(2 * GROUP - 1):
-                whole = whole + tot_z[d]
-            tot2[...] = whole
             to_come_x = GROUP - 1 - at_x0
 
             @pl.when(jnp.logical_and(jnp.logical_not(wide), to_come_x > 0))
             def _():
                 pl.semaphore_wait(sem_line, to_come_x)
 
+            wait(tot_z, sem_got.at[TOTAL])
+            early = tot[...] + tot_z[0] + tot_z[1] + tot_z[2]
+            tot2[0] = early
+
+            @pl.when(at_x0 > 0)
+            def _():
+                send(tot2.at[0], tot_x.at[3 - at_x0], TOTAL_X, TOTALS, (member, t))
+
+            wait(tot_l, sem_got.at[TOTAL_L])
+            tot2[1] = early + tot_l[0] + tot_l[1] + tot_l[2] + tot_l[3]
             for d in (1, 2, 3):
-                send(tot2, tot_x.at[d - 1], TOTAL_X, TOTALS, at_x(d))
+
+                @pl.when(at_x0 + d != SHARDS // (2 * GROUP))
+                def _():
+                    send(tot2.at[1], tot_x.at[d - 1], TOTAL_X, TOTALS, at_x(d))
 
     with jax.named_scope("waitchip"):
         wait(chip_in, sem_got.at[CHIP])
@@ -275,7 +294,16 @@
         @pl.when(hub)
         def _():
             wait(tot_x, sem_got.at[TOTAL_X])
-            grand[...] = tot2[...] + tot_x[0] + tot_x[1] + tot_x[2]
+            grand[...] = tot2[1] + tot_x[0] + tot_x[1] + tot_x[2]
+
+            @pl.when(at_x0 == 0)
+            def _():
+                wait(tot_f, sem_got.at[TOTAL_F])
+                whole = grand[...]
+                for i in range(3 * GROUP):
+                    whole = whole + tot_f[i]
+                grand[...] = whole
+
             send(grand, grand, GRAND, TOTALS, at_other(GROUP - 1 - member))
             send(grand, grand, GRAND, TOTALS, at_other(GROUP - member))
             send(grand, grand, GRAND, TOTALS, at_group(GROUP - 1))
@@ -359,11 +387,17 @@
     with jax.named_scope("waitsend"):
         @pl.when(hub)
         def _():
-            wait(tot_z, sem_sent.at[TOTALS])
-
-        @pl.when(jnp.logical_not(hub))
-        def _():
-            wait(tot_z.at[pl.ds(0, 2)], sem_sent.at[TOTALS])
+            wait(tot_f.at[pl.ds(0, 7)], sem_sent.at[TOTALS])
+
+        direct = jnp.logical_and(late == 1, at_x0 > 0)
+
+        @pl.when(direct)
+        def _():
+            wait(tot_f.at[pl.ds(0, 4)], sem_sent.at[TOTALS])
+
+        @pl.when(jnp.logical_not(jnp.logical_or(hub, direct)))
+        def _():
+            wait(tot_f.at[pl.ds(0, 2)], sem_sent.at[TOTALS])
 
         wait(masked.at[pl.ds(0, 3), 0], sem_sent.at[COLUMNS])
         wait(masked.at[0, 0, 0], sem_sent.at[PROBS])
@@ -392,13 +426,15 @@
             pltpu.VMEM((LAYERS, 2, HERE, HALF), F32),
             *[pltpu.VMEM((2, LAYERS, HERE, HALF), BF16)] * 4,
             pltpu.VMEM((8, LANES), F32),
-            pltpu.VMEM((2 * GROUP - 1, 8, LANES), F32),
-            pltpu.VMEM((8, LANES), F32),
+            pltpu.VMEM((GROUP - 1, 8, LANES), F32),
+            pltpu.VMEM((GROUP, 8, LANES), F32),
+            pltpu.VMEM((2, 8, LANES), F32),
             pltpu.VMEM((3, 8, LANES), F32),
+            pltpu.VMEM((3 * GROUP, 8, LANES), F32),
             pltpu.VMEM((8, LANES), F32),
             dma((10,)),
             dma((4,)),
-            dma((10,)),
+            dma((12,)),
             dma((LAYERS,)),
             pltpu.SemaphoreType.REGULAR,
             pltpu.SemaphoreType.REGULAR,

time: 25.1 us -> 24.4 us (0.972)
  the two profiles are of different devices: /device:TPU:0 before, /device:TPU:98 now
where the time goes in v6:
time: 24.4 us; the launch traced here: 24.3 us
  Pallas kernels  23.5 us (96%)
  local copies, waits for them, and re-layouts  0.8 us (3%)
    pallas_call x1, Pallas kernels, on_device(): pl.pallas_call(kernel, out_shape=jax.ShapeDtypeStruct((LAYERS, HERE, 2 *...  23.5 us
    unnamed x1, local copies, waits for them, and re-layouts  0.8 us

profile of v6, /device:TPU:98, one launch (start us, length us, event | category | flops | bytes accessed | tf_op | source)
XLA Modules:
  0.0 24.3 jit_solution(9420697597968553506)
XLA Ops:
  0.0 23.5 %shard_map.37 = bf16[4,16,4096]{2,1,0:T(8,128)(2,1)S(1)} custom-call(bf16[1,4,16,16384]{3,2,1,0:T(8,128)(2,1)} %delta.1, s32[1,4,16,16384]{3,2,1,0:T(8,128)} %score.1, s32[1,4,8]{2,1,0:T(4,128)} %limit_in.1), custom_call_target="tpu_custom_call" | custom-call | tf_op jit(solution)/shard_map/pallas_call | solution.py:410
  23.5 0.8 %copy.5 = bf16[4,16,4096]{2,1,0:T(8,128)(2,1)} copy(bf16[4,16,4096]{2,1,0:T(8,128)(2,1)S(1)} %shard_map.37) | data formatting | bytes 1048576

commit v7 on v6

--- a/solution.py
+++ b/solution.py
@@ -14,6 +14,7 @@
 TASKS = 4
 SHARDS = 32
 GROUP = 4
+LINE = 4
 HERE = 16
 HALF = 2048
 LANES = 128
@@ -101,13 +102,14 @@
     @pl.when(hub)
     def _():
         for d in (1, 2, 3):
-            pl.when(jnp.logical_or(wide, at_x0 + d < SHARDS // (2 * GROUP)))(functools.partial(greet, at_x(d)))
+            pl.when(jnp.logical_or(wide, at_x0 + d < LINE))(functools.partial(greet, at_x(d)))
         for m in range(GROUP):
             greet(at_other(m))
 
-        @pl.when(at_x0 == 0)
-        def _():
-            for x in range(1, SHARDS // (2 * GROUP)):
+        for x in range(1, LINE):
+
+            @pl.when(at_x0 < x)
+            def _():
                 for m in range(GROUP):
                     greet(((2 * x + 1) * GROUP + m, t))
 
@@ -184,7 +186,7 @@
             mask_near()
 
     with jax.named_scope("bar"):
-        met = jnp.where(wide, GROUP - 1, member) + 2 * late * jnp.where(at_x0 > 0, 2, 1) + jnp.where(hub, jnp.where(wide, GROUP - 1, at_x0), 0)
+        met = jnp.where(wide, GROUP - 1, member) + 2 * late * (1 + at_x0) + jnp.where(hub, jnp.where(wide, GROUP - 1, at_x0), 0)
         pl.semaphore_wait(barrier, 2 + met)
     send_far(0)
 
@@ -221,10 +223,13 @@
         for m in (1, 3):
             send(tot, tot_l.at[member], TOTAL_L, TOTALS, at_other(m))
 
-        @pl.when(at_x0 > 0)
-        def _():
-            for m in (1, 3):
-                send(tot, tot_f.at[GROUP * (at_x0 - 1) + member], TOTAL_F, TOTALS, (m, t))
+        for x in range(LINE - 1):
+
+            @pl.when(at_x0 > x)
+            def _():
+                for m in (1, 3):
+                    slot = GROUP * (at_x0 - x - 1) + member
+                    send(tot, tot_f.at[slot], TOTAL_F, TOTALS, (2 * GROUP * x + m, t))
 
     with jax.named_scope("near"):
 
@@ -273,15 +278,17 @@
             early = tot[...] + tot_z[0] + tot_z[1] + tot_z[2]
             tot2[0] = early
 
-            @pl.when(at_x0 > 0)
-            def _():
-                send(tot2.at[0], tot_x.at[3 - at_x0], TOTAL_X, TOTALS, (member, t))
+            for d in (1, 2, 3):
+
+                @pl.when(at_x0 + d >= LINE)
+                def _():
+                    send(tot2.at[0], tot_x.at[d - 1], TOTAL_X, TOTALS, at_x(d))
 
             wait(tot_l, sem_got.at[TOTAL_L])
             tot2[1] = early + tot_l[0] + tot_l[1] + tot_l[2] + tot_l[3]
             for d in (1, 2, 3):
 
-                @pl.when(at_x0 + d != SHARDS // (2 * GROUP))
+                @pl.when(at_x0 + d < LINE)
                 def _():
                     send(tot2.at[1], tot_x.at[d - 1], TOTAL_X, TOTALS, at_x(d))
 
@@ -296,13 +303,16 @@
             wait(tot_x, sem_got.at[TOTAL_X])
             grand[...] = tot2[1] + tot_x[0] + tot_x[1] + tot_x[2]
 
-            @pl.when(at_x0 == 0)
-            def _():
-                wait(tot_f, sem_got.at[TOTAL_F])
-                whole = grand[...]
-                for i in range(3 * GROUP):
-                    whole = whole + tot_f[i]
-                grand[...] = whole
+            for x in range(LINE - 1):
+
+                @pl.when(at_x0 == x)
+                def _():
+                    count = GROUP * (LINE - 1 - x)
+                    wait(tot_f.at[pl.ds(0, count)], sem_got.at[TOTAL_F])
+                    whole = grand[...]
+                    for i in range(count):
+                        whole = whole + tot_f[i]
+                    grand[...] = whole
 
             send(grand, grand, GRAND, TOTALS, at_other(GROUP - 1 - member))
             send(grand, grand, GRAND, TOTALS, at_other(GROUP - member))
@@ -389,13 +399,13 @@
         def _():
             wait(tot_f.at[pl.ds(0, 7)], sem_sent.at[TOTALS])
 
-        direct = jnp.logical_and(late == 1, at_x0 > 0)
-
-        @pl.when(direct)
-        def _():
-            wait(tot_f.at[pl.ds(0, 4)], sem_sent.at[TOTALS])
-
-        @pl.when(jnp.logical_not(jnp.logical_or(hub, direct)))
+        for x in range(LINE):
+
+            @pl.when(jnp.logical_and(late == 1, at_x0 == x))
+            def _():
+                wait(tot_f.at[pl.ds(0, 2 * (x + 1))], sem_sent.at[TOTALS])
+
+        @pl.when(jnp.logical_and(late == 0, core == 0))
         def _():
             wait(tot_f.at[pl.ds(0, 2)], sem_sent.at[TOTALS])
 

time: 24.4 us -> 24 us (0.984)
  the two profiles are of different devices: /device:TPU:98 before, /device:TPU:0 now
where the time goes in v7:
time: 24 us; the launch traced here: 23.9 us
  Pallas kernels  23.1 us (96%)
  local copies, waits for them, and re-layouts  0.8 us (3%)
    pallas_call x1, Pallas kernels, on_device(): pl.pallas_call(kernel, out_shape=jax.ShapeDtypeStruct((LAYERS, HERE, 2 *...  23.1 us
    unnamed x1, local copies, waits for them, and re-layouts  0.8 us

profile of v7, /device:TPU:0, one launch (start us, length us, event | category | flops | bytes accessed | tf_op | source)
XLA Modules:
  0.0 23.9 jit_solution(9323863174773445292)
XLA Ops:
  0.0 23.1 %shard_map.37 = bf16[4,16,4096]{2,1,0:T(8,128)(2,1)S(1)} custom-call(bf16[1,4,16,16384]{3,2,1,0:T(8,128)(2,1)} %delta.1, s32[1,4,16,16384]{3,2,1,0:T(8,128)} %score.1, s32[1,4,8]{2,1,0:T(4,128)} %limit_in.1), custom_call_target="tpu_custom_call" | custom-call | tf_op jit(solution)/shard_map/pallas_call | solution.py:420
  23.1 0.8 %copy.5 = bf16[4,16,4096]{2,1,0:T(8,128)(2,1)} copy(bf16[4,16,4096]{2,1,0:T(8,128)(2,1)S(1)} %shard_map.37) | data formatting | bytes 1048576

commit v8 on v7

--- a/solution.py
+++ b/solution.py
@@ -66,7 +66,7 @@
     def wait(ref, sem):
         pltpu.make_async_copy(ref, ref, sem).wait()
 
-    PAIR, CHIP, WHOLE, TOTAL, TOTAL_L, TOTAL_X, TOTAL_F, GRAND, PROB_F, PROB_Y, NEAR, FAR = range(12)
+    PAIR, CHIP, WHOLE, TOTAL, TOTAL_L, TOTAL_X, TOTAL_F, GRAND, PROB_F, PROB_Y, PROB_P, NEAR, FAR = range(13)
     COLUMNS, TOTALS, PROBS, ENTRIES = range(4)
 
     barrier = pltpu.get_barrier_semaphore()
@@ -350,7 +350,9 @@
     for l in range(LAYERS - HELD, LAYERS):
         send_near(l)
     for d, owner, h in ((1, up, 1), (3, down, 0)):
-        send(prob.at[owner, :, h], prob_in.at[h], PROB_Y, PROBS, at_task(d))
+        pl.when(core == 1 - h)(
+            functools.partial(send, prob.at[owner, :, h], prob_in.at[h], PROB_Y, PROBS, at_task(d))
+        )
 
     with jax.named_scope("own"):
         for l in range(LAYERS):
@@ -374,9 +376,13 @@
             send(joint.at[h, l], joint_in.at[h, l], None, ENTRIES, at_task(3 if h else 1), sem_j.at[l])
 
     with jax.named_scope("waitpy"):
-        wait(prob_in, sem_got.at[PROB_Y])
+        mine = 1 - core
+        wait(prob_in.at[mine], sem_got.at[PROB_Y])
+        send(prob_in.at[mine], prob_in.at[mine], PROB_P, PROBS, at_group(1 - 2 * core + GROUP))
     with jax.named_scope("waitraw"):
         wait(raw_in, sem_got.at[NEAR])
+    with jax.named_scope("waitpp"):
+        wait(prob_in.at[core], sem_got.at[PROB_P])
     with jax.named_scope("raw"):
         for l in range(LAYERS):
             for h in range(2):
@@ -444,7 +450,7 @@
             pltpu.VMEM((8, LANES), F32),
             dma((10,)),
             dma((4,)),
-            dma((12,)),
+            dma((13,)),
             dma((LAYERS,)),
             pltpu.SemaphoreType.REGULAR,
             pltpu.SemaphoreType.REGULAR,

time: 24 us -> 23.8 us (level)
  no operation moved by 1% of the time
where the time goes in v8:
time: 23.8 us; the launch traced here: 23.7 us
  Pallas kernels  22.9 us (96%)
  local copies, waits for them, and re-layouts  0.8 us (3%)
    pallas_call x1, Pallas kernels, on_device(): pl.pallas_call(kernel, out_shape=jax.ShapeDtypeStruct((LAYERS, HERE, 2 *...  22.9 us
    unnamed x1, local copies, waits for them, and re-layouts  0.8 us

profile of v8, /device:TPU:0, one launch (start us, length us, event | category | flops | bytes accessed | tf_op | source)
XLA Modules:
  0.0 23.7 jit_solution(9557440847258617823)
XLA Ops:
  0.0 22.9 %shard_map.37 = bf16[4,16,4096]{2,1,0:T(8,128)(2,1)S(1)} custom-call(bf16[1,4,16,16384]{3,2,1,0:T(8,128)(2,1)} %delta.1, s32[1,4,16,16384]{3,2,1,0:T(8,128)} %score.1, s32[1,4,8]{2,1,0:T(4,128)} %limit_in.1), custom_call_target="tpu_custom_call" | custom-call | tf_op jit(solution)/shard_map/pallas_call | solution.py:426
  22.9 0.8 %copy.5 = bf16[4,16,4096]{2,1,0:T(8,128)(2,1)} copy(bf16[4,16,4096]{2,1,0:T(8,128)(2,1)S(1)} %shard_map.37) | data formatting | bytes 1048576

commit v9 on v8

--- a/solution.py
+++ b/solution.py
@@ -261,7 +261,7 @@
     with jax.named_scope("waitpair"):
         wait(pair_in, sem_got.at[PAIR])
     half[...] = sums[core] + pair_in[...]
-    chip_out[...] = half[...]
+    chip_out[...] = half[...].astype(BF16)
     send(chip_out, chip_in, CHIP, COLUMNS, at_group(2))
 
     with jax.named_scope("totals1"):
@@ -294,7 +294,7 @@
 
     with jax.named_scope("waitchip"):
         wait(chip_in, sem_got.at[CHIP])
-    half[...] = chip_out[...] + chip_in[...]
+    half[...] = half[...] + chip_in[...].astype(F32)
     send(half, half_in, WHOLE, COLUMNS, at_group(1 - 2 * core + GROUP))
     with jax.named_scope("totals2"):
 
@@ -415,7 +415,7 @@
         def _():
             wait(tot_f.at[pl.ds(0, 2)], sem_sent.at[TOTALS])
 
-        wait(masked.at[pl.ds(0, 3), 0], sem_sent.at[COLUMNS])
+        wait(dbuf.at[0, :, pl.ds(0, 5 * HALF)], sem_sent.at[COLUMNS])
         wait(masked.at[0, 0, 0], sem_sent.at[PROBS])
         wait(masked.at[pl.ds(0, 3)], sem_sent.at[ENTRIES])
 
@@ -435,7 +435,8 @@
             pltpu.VMEM((TASKS, LAYERS, 2, HERE, HALF), BF16),
             pltpu.VMEM((2, TASKS, LAYERS, PARTS, LANES), F32),
             pltpu.VMEM((TASKS, LAYERS, PARTS, LANES), F32),
-            *[pltpu.VMEM((TASKS, LAYERS, PARTS, LANES), F32)] * 4,
+            *[pltpu.VMEM((TASKS, LAYERS, PARTS, LANES), BF16)] * 2,
+            *[pltpu.VMEM((TASKS, LAYERS, PARTS, LANES), F32)] * 2,
             pltpu.VMEM((TASKS, LAYERS, 2, PARTS, LANES), BF16),
             pltpu.VMEM((TASKS, LAYERS, 2, PARTS, LANES), F32),
             *[pltpu.VMEM((2, LAYERS, PARTS, LANES), BF16)] * 2,

time: 23.8 us -> 23.8 us (level)
  no operation moved by 1% of the time
where the time goes in v9:
time: 23.8 us; the launch traced here: 23.7 us
  Pallas kernels  22.9 us (96%)
  local copies, waits for them, and re-layouts  0.8 us (3%)
    pallas_call x1, Pallas kernels, on_device(): pl.pallas_call(kernel, out_shape=jax.ShapeDtypeStruct((LAYERS, HERE, 2 *...  22.9 us
    unnamed x1, local copies, waits for them, and re-layouts  0.8 us

profile of v9, /device:TPU:0, one launch (start us, length us, event | category | flops | bytes accessed | tf_op | source)
XLA Modules:
  0.0 23.7 jit_solution(6675386287376763008)
XLA Ops:
  0.0 22.9 %shard_map.37 = bf16[4,16,4096]{2,1,0:T(8,128)(2,1)S(1)} custom-call(bf16[1,4,16,16384]{3,2,1,0:T(8,128)(2,1)} %delta.1, s32[1,4,16,16384]{3,2,1,0:T(8,128)} %score.1, s32[1,4,8]{2,1,0:T(4,128)} %limit_in.1), custom_call_target="tpu_custom_call" | custom-call | tf_op jit(solution)/shard_map/pallas_call | solution.py:426
  22.9 0.8 %copy.5 = bf16[4,16,4096]{2,1,0:T(8,128)(2,1)} copy(bf16[4,16,4096]{2,1,0:T(8,128)(2,1)S(1)} %shard_map.37) | data formatting | bytes 1048576
